TPU v7x, 128 devices: a whole 4x4x4 slice. The times are simulated.
128 devices in a mesh: batch: 8 (over x, core), rows: 16 (over z, y).
Axes of the slice: x: 4, y: 4, z: 4, core: 2. Of those that a mesh axis runs over, the one named last changes fastest.
Arguments:
- feat_quarter: bfloat16 [8, 256, 512, 256], P('batch', 'rows'), may hold values from -12 to 12
- feat_eighth: bfloat16 [8, 128, 256, 256], P('batch', 'rows'), may hold values from -12 to 12
- feat_sixteenth: bfloat16 [8, 64, 128, 256], P('batch', 'rows'), may hold values from -12 to 12
- feat_thirty: bfloat16 [8, 32, 64, 256], P('batch', 'rows'), may hold values from -12 to 12
- labels: int32 [8, 256, 512], P('batch', 'rows'), may hold values from 0 to 255, as said below
- first_weights: bfloat16 [4, 3, 3, 256, 128], replicated, may hold values from -0.125 to 0.125
- inner_weights: bfloat16 [3, 3, 3, 128, 128], replicated, may hold values from -0.1875 to 0.1875
- norm_gain: float32 [7, 128], replicated, may hold values from 0.1 to 1.9
- norm_shift: float32 [7, 128], replicated, may hold values from -3 to 3
- class_weight: bfloat16 [128, 19], replicated, may hold values from -0.5 to 0.5
- class_bias: float32 [19], replicated, may hold values from -3 to 3
Outputs:
- logits: bfloat16 [8, 19, 256, 512], P('batch', None, 'rows')
- mean_loss: float32 [], replicated
Inputs may be any that keep to these rules, and one draw needn't show every extreme that they name: `labels`: values 0 to 18 name classes; 255 marks a pixel without a label.
All inputs are finite; a program needn't handle non-finite values.
Results may differ from a plain program's by a relative error of at most 0.008.
Values may be sent and summed in bfloat16 or wider, within the bound.
A program may use at most 128 MiB of HBM per device.

v0:
```python
import functools

import jax
import jax.numpy as jnp
from jax import lax
from jax.experimental import pallas as pl
from jax.experimental.pallas import tpu as pltpu
from jax.sharding import PartitionSpec as P

MESH = pl.DeviceIdType.MESH
FLOOR = 0.05
CLASSES = 19
F32 = jnp.float32
BF16 = jnp.bfloat16


def group_total(tile):
    lane = lax.broadcasted_iota(jnp.int32, tile.shape, 1)
    tile = tile + jnp.where(lane % 2 == 0, pltpu.roll(tile, 127, 1), pltpu.roll(tile, 1, 1))
    return tile + jnp.where(lane % 4 < 2, pltpu.roll(tile, 126, 1), pltpu.roll(tile, 2, 1))


def double_matrix(width, out_axis):
    shape = (2 * width, width) if out_axis == 0 else (width, 2 * width)
    out = lax.broadcasted_iota(jnp.int32, shape, out_axis)
    src = lax.broadcasted_iota(jnp.int32, shape, 1 - out_axis)
    half = out // 2
    other = jnp.clip(half + 2 * (out % 2) - 1, 0, width - 1)
    return jnp.where(src == half, 0.75, 0.0) + jnp.where(src == other, 0.25, 0.0)


def kernel(
    nb, nr,
    xq_hbm, x8_hbm, x16_hbm, x32_hbm, lab_hbm, fw_hbm, iw_hbm, gain_hbm, shift_hbm, cw_hbm, cb_hbm,
    out_ref, loss_ref,
    xq, x8, x16, x32, lab, fw, iw, gain, shift, cw, cb,
    yq, y8, y16, y32, y4, y5, y6,
    a16, a32, a5, in4, in5, in6,
    p512, p256, p128, p64,
    u64, u128, u256, cwf, wct, bias,
    qt, zt, zc, sums, picks, tall,
    stats, loss_rows, loss_batch,
    local_sem, halo_send, halo_recv, stat_send, stat_recv, loss_send, loss_recv,
):
    pos = lax.axis_index("rows")
    bat = lax.axis_index("batch")
    last = nr - 1

    def local(src, dst, index):
        return pltpu.make_async_copy(src, dst, local_sem.at[index])

    copies = {
        "fw3": local(fw_hbm.at[3], fw.at[3], 0),
        "x32": local(x32_hbm.at[0], x32.at[pl.ds(3, 2)], 1),
        "fw0": local(fw_hbm.at[0], fw.at[0], 2),
        "xqa": local(xq_hbm.at[0, pl.ds(0, 8)], xq.at[pl.ds(1, 8)], 3),
        "xqb": local(xq_hbm.at[0, pl.ds(8, 8)], xq.at[pl.ds(9, 8)], 4),
        "gain": local(gain_hbm, gain, 5),
        "shift": local(shift_hbm, shift, 6),
        "cw": local(cw_hbm, cw, 7),
        "cb": local(cb_hbm, cb, 8),
        "fw2": local(fw_hbm.at[2], fw.at[2], 9),
        "x16": local(x16_hbm.at[0], x16.at[pl.ds(3, 4)], 10),
        "iw": local(iw_hbm, iw, 11),
        "fw1": local(fw_hbm.at[1], fw.at[1], 12),
        "x8": local(x8_hbm.at[0], x8.at[pl.ds(2, 8)], 13),
        "lab": local(lab_hbm.at[0], lab, 14),
    }

    barrier = pltpu.get_barrier_semaphore()

    def greet_row(k, carry):
        pl.semaphore_signal(
            barrier, inc=1, device_id={"rows": lax.rem(pos + k, nr)}, device_id_type=MESH
        )
        return carry

    def greet_batch(k, carry):
        pl.semaphore_signal(
            barrier, inc=1, device_id={"batch": lax.rem(bat + k, nb)}, device_id_type=MESH
        )
        return carry

    lax.fori_loop(1, nr, greet_row, 0)
    lax.fori_loop(1, nb, greet_batch, 0)
    for name in ("fw0", "xqa", "xqb", "x32", "fw3", "cw", "cb", "gain", "shift", "fw2", "x16", "iw",
                 "fw1", "x8", "lab"):
        copies[name].start()

    m64 = double_matrix(64, 0)
    u64[:, 0:64] = 0.75 * m64
    u64[:, 64:128] = 0.25 * m64
    m128 = double_matrix(128, 0)
    u128[:, 0:128] = (0.75 * m128).astype(BF16)
    u128[:, 128:256] = (0.25 * m128).astype(BF16)
    u256[...] = double_matrix(256, 1).astype(BF16)
    for scratch, width in ((p512, 512), (p256, 256), (p128, 128), (p64, 64)):
        rows = scratch.shape[1]
        scratch[:, :, 0:8, :] = jnp.zeros((2, rows, 8, 128), F32)
        scratch[:, :, width + 8 : width + 16, :] = jnp.zeros((2, rows, 8, 128), F32)

    @pl.when(pos == 0)
    def _():
        xq[0] = jnp.zeros_like(xq[0])
        x8[0:2] = jnp.zeros_like(x8[0:2])
        x16[0:3] = jnp.zeros_like(x16[0:3])
        x32[0:3] = jnp.zeros_like(x32[0:3])

    @pl.when(pos == 1)
    def _():
        x32[0] = jnp.zeros_like(x32[0])

    @pl.when(pos == last)
    def _():
        xq[17] = jnp.zeros_like(xq[17])
        x8[10:12] = jnp.zeros_like(x8[10:12])
        x16[7:10] = jnp.zeros_like(x16[7:10])
        x32[5:8] = jnp.zeros_like(x32[5:8])

    @pl.when(pos == last - 1)
    def _():
        x32[7] = jnp.zeros_like(x32[7])

    copies["cw"].wait()
    copies["cb"].wait()
    cwf[...] = jnp.zeros_like(cwf)
    cwf[:, 0:CLASSES] = cw[...].astype(F32)
    wct[...] = jnp.transpose(cwf[...])[0:32].astype(BF16)
    cwf[...] = jnp.zeros_like(cwf)
    cwf[0:1, 0:CLASSES] = cb[...]
    bias[...] = jnp.broadcast_to(jnp.transpose(cwf[...])[0:32, 0:1], (32, 512))

    pl.semaphore_wait(barrier, nr - 1 + nb - 1)

    def halo(src, dst, index, step):
        return pltpu.make_async_remote_copy(
            src_ref=src, dst_ref=dst, send_sem=halo_send.at[index], recv_sem=halo_recv.at[index],
            device_id={"rows": pos + step}, device_id_type=MESH,
        )

    def halos(name):
        if name == "t1":
            return (halo(x32_hbm.at[0], x32.at[pl.ds(1, 2)], 0, 1),
                    halo(x32_hbm.at[0], x32.at[pl.ds(5, 2)], 1, -1), 1)
        if name == "t2":
            return (halo(x32_hbm.at[0, pl.ds(1, 1)], x32.at[pl.ds(0, 1)], 2, 2),
                    halo(x32_hbm.at[0, pl.ds(0, 1)], x32.at[pl.ds(7, 1)], 3, -2), 2)
        if name == "s":
            return (halo(x16_hbm.at[0, pl.ds(1, 3)], x16.at[pl.ds(0, 3)], 4, 1),
                    halo(x16_hbm.at[0, pl.ds(0, 3)], x16.at[pl.ds(7, 3)], 5, -1), 1)
        if name == "e":
            return (halo(x8_hbm.at[0, pl.ds(6, 2)], x8.at[pl.ds(0, 2)], 6, 1),
                    halo(x8_hbm.at[0, pl.ds(0, 2)], x8.at[pl.ds(10, 2)], 7, -1), 1)
        return (halo(xq_hbm.at[0, pl.ds(15, 1)], xq.at[pl.ds(0, 1)], 8, 1),
                halo(xq_hbm.at[0, pl.ds(0, 1)], xq.at[pl.ds(17, 1)], 9, -1), 1)

    def halo_start(name):
        down, up, step = halos(name)
        pl.when(pos + step <= last)(down.start)
        pl.when(pos - step >= 0)(up.start)

    def halo_wait(name):
        down, up, step = halos(name)
        pl.when(pos - step >= 0)(down.wait_recv)
        pl.when(pos + step <= last)(up.wait_recv)

    def halo_sent(name):
        down, up, step = halos(name)
        pl.when(pos + step <= last)(down.wait_send)
        pl.when(pos - step >= 0)(up.wait_send)

    for name in ("t1", "t2", "s", "e", "q"):
        halo_start(name)

    def conv(x_ref, in_off, w_ref, y_ref, first, count, width, per_step, pad):
        depth = x_ref.shape[2]

        def step(i, carry):
            row = first + i * per_step
            lhs = jnp.concatenate(
                [x_ref[pl.ds(in_off + row + dr, per_step)].reshape(per_step * width, depth)
                 for dr in range(3)], axis=1)
            rhs = jnp.concatenate(
                [jnp.concatenate([w_ref[dr, dc] for dc in range(3)], axis=1) for dr in range(3)],
                axis=0)
            part = jnp.dot(lhs, rhs, preferred_element_type=F32)
            shape = (per_step, width, 128)
            pad[0, :, 8 : 8 + width, :] = part[:, 0:128].reshape(shape)
            pad[1, :, 8 : 8 + width, :] = part[:, 256:384].reshape(shape)
            y_ref[pl.ds(row, per_step)] = (
                part[:, 128:256].reshape(shape)
                + pad[0, :, 7 : 7 + width, :]
                + pad[1, :, 9 : 9 + width, :]
            )
            return carry

        lax.fori_loop(0, count // per_step, step, 0)

    def moments(y_ref, first, count, width, layer):
        def add(i, acc):
            return acc + jnp.sum(y_ref[first + i].reshape(width // 8, 8, 128), axis=0)

        total = lax.fori_loop(0, count, add, jnp.zeros((8, 128), F32))
        total = jnp.broadcast_to(jnp.sum(total, axis=0, keepdims=True), (8, 128))
        mean = group_total(total) * (1.0 / (count * width * 4))

        def add_square(i, acc):
            off = y_ref[first + i].reshape(width // 8, 8, 128) - mean[None]
            return acc + jnp.sum(off * off, axis=0)

        square = lax.fori_loop(0, count, add_square, jnp.zeros((8, 128), F32))
        square = jnp.broadcast_to(jnp.sum(square, axis=0, keepdims=True), (8, 128))
        square = group_total(square)
        sub = lax.broadcasted_iota(jnp.int32, (8, 128), 0)
        stats[layer, pos] = jnp.where(sub == 0, mean, square)

        def send(k, carry):
            stat_copy(layer, lax.rem(pos + k, nr)).start()
            return carry

        lax.fori_loop(1, nr, send, 0)

    def stat_copy(layer, peer):
        return pltpu.make_async_remote_copy(
            src_ref=stats.at[layer, pos], dst_ref=stats.at[layer, pos],
            send_sem=stat_send.at[layer], recv_sem=stat_recv.at[layer],
            device_id={"rows": peer}, device_id_type=MESH,
        )

    def tiles_wait(ref, sem):
        pltpu.make_async_copy(ref, ref, sem).wait()

    def scales(layer, local_count):
        tiles_wait(stats.at[layer, pl.ds(0, nr - 1)], stat_recv.at[layer])
        every = [stats[layer, i] for i in range(nr)]
        total = functools.reduce(lambda a, b: a + b, every)
        mean = total[0:1] * (1.0 / nr)
        spread = [(tile[0:1] - mean) * (tile[0:1] - mean) for tile in every]
        square = total[1:2] + local_count * functools.reduce(lambda a, b: a + b, spread)
        var = square * (1.0 / (nr * local_count))
        factor = gain[pl.ds(layer, 1), :] * lax.rsqrt(var + FLOOR)
        return mean, factor, shift[pl.ds(layer, 1), :]

    def activate(values, scale):
        mean, factor, offset = scale
        return jnp.maximum((values - mean) * factor + offset, 0.0).astype(BF16)

    def normalize(y_ref, a_ref, scale, rows, top, bottom):
        for r in range(rows):
            a_ref[r] = activate(y_ref[r], scale)

        @pl.when(pos == 0)
        def _():
            a_ref[top] = a_ref[top + 1]

        @pl.when(pos == last)
        def _():
            a_ref[bottom] = a_ref[bottom - 1]

    def double(a_ref, u_ref, in_ref, pairs, base, width):
        top_row = a_ref.shape[0] - 1
        for j in range(pairs):
            k = base + j
            mid = a_ref[k]
            rhs = jnp.concatenate(
                [jnp.concatenate([mid, mid], axis=1),
                 jnp.concatenate([a_ref[max(k - 1, 0)], a_ref[min(k + 1, top_row)]], axis=1)],
                axis=0)
            both = jnp.dot(u_ref[...].astype(BF16), rhs, preferred_element_type=F32).astype(BF16)
            in_ref[2 * j] = both[:, 0:128]
            in_ref[2 * j + 1] = both[:, 128:256]

    def clear_outside(in_ref, top_rows, bottom_row):
        @pl.when(pos == 0)
        def _():
            in_ref[0:top_rows] = jnp.zeros_like(in_ref[0:top_rows])

        @pl.when(pos == last)
        def _():
            rest = in_ref.shape[0] - bottom_row
            in_ref[bottom_row:] = jnp.zeros((rest,) + in_ref.shape[1:], BF16)

    nt = (((1,), (1,)), ((), ()))

    copies["fw0"].wait()
    copies["xqa"].wait()
    conv(xq, 0, fw.at[0], yq, 1, 6, 512, 2, p512)

    copies["fw3"].wait()
    copies["x32"].wait()
    halo_wait("t1")
    halo_wait("t2")
    conv(x32, 0, fw.at[3], y32, 0, 6, 64, 6, p64)
    moments(y32, 2, 2, 64, 3)

    copies["fw2"].wait()
    copies["x16"].wait()
    halo_wait("s")
    conv(x16, 0, fw.at[2], y16, 0, 8, 128, 4, p128)
    moments(y16, 2, 4, 128, 2)

    copies["xqb"].wait()
    conv(xq, 0, fw.at[0], yq, 7, 4, 512, 2, p512)

    copies["gain"].wait()
    copies["shift"].wait()
    copies["iw"].wait()
    normalize(y32, a32, scales(3, 2 * 64 * 4), 6, 1, 4)
    double(a32, u64, in5, 6, 0, 64)
    clear_outside(in5, 4, 8)
    conv(in5, 1, iw.at[1], y5, 0, 8, 128, 4, p128)
    moments(y5, 2, 4, 128, 5)

    normalize(y16, a16, scales(2, 4 * 128 * 4), 8, 1, 6)
    double(a16, u128, in4, 6, 1, 128)
    clear_outside(in4, 2, 10)
    conv(in4, 0, iw.at[0], y4, 0, 10, 256, 2, p256)
    moments(y4, 1, 8, 256, 4)

    copies["fw1"].wait()
    copies["x8"].wait()
    halo_wait("e")
    conv(x8, 0, fw.at[1], y8, 0, 10, 256, 2, p256)
    moments(y8, 1, 8, 256, 1)

    normalize(y5, a5, scales(5, 4 * 128 * 4), 8, 1, 6)
    double(a5, u128, in6, 6, 1, 128)
    clear_outside(in6, 2, 10)
    conv(in6, 0, iw.at[2], y6, 0, 10, 256, 2, p256)
    moments(y6, 1, 8, 256, 6)

    conv(xq, 0, fw.at[0], yq, 11, 4, 512, 2, p512)
    halo_wait("q")

    def edge(i, carry):
        row = i * 15
        lhs = jnp.concatenate([xq[row + dr] for dr in range(3)], axis=1)
        rhs = jnp.concatenate(
            [jnp.concatenate([fw[0, dr, dc] for dc in range(3)], axis=1) for dr in range(3)], axis=0)
        part = jnp.dot(lhs, rhs, preferred_element_type=F32)
        p512[0, 0, 8:520, :] = part[:, 0:128]
        p512[1, 0, 8:520, :] = part[:, 256:384]
        yq[row] = part[:, 128:256] + p512[0, 0, 7:519, :] + p512[1, 0, 9:521, :]
        return carry

    lax.fori_loop(0, 2, edge, 0)
    moments(yq, 0, 16, 512, 0)

    def project(y_ref, scale, fresh):
        def step(r, carry):
            act = activate(y_ref[r], scale)
            part = lax.dot_general(wct[...], act, nt, preferred_element_type=F32)
            zt[r] = part if fresh else zt[r] + part
            return carry

        lax.fori_loop(0, 10, step, 0)

    project(y4, scales(4, 8 * 256 * 4), True)
    project(y8, scales(1, 8 * 256 * 4), False)
    project(y6, scales(6, 8 * 256 * 4), False)

    @pl.when(pos == 0)
    def _():
        zt[0] = zt[1]

    @pl.when(pos == last)
    def _():
        zt[9] = zt[8]

    flat = zt[...].reshape(320, 256)
    high = flat.astype(BF16)
    low = (flat - high.astype(F32)).astype(BF16)
    zc[...] = (
        jnp.dot(high, u256[...], preferred_element_type=F32)
        + jnp.dot(low, u256[...], preferred_element_type=F32)
    ).reshape(10, 32, 512)

    scale_q = scales(0, 16 * 512 * 4)
    copies["lab"].wait()

    def finish(r, carry):
        act = activate(yq[r], scale_q)
        main = lax.dot_general(wct[...], act, nt, preferred_element_type=F32)
        half = r // 2
        near = half + 2 * (r % 2)
        score = main + 0.75 * zc[half + 1] + 0.25 * zc[near] + bias[...]
        kind = lax.broadcasted_iota(jnp.int32, (32, 512), 0)
        grown = jnp.where(kind < CLASSES, jnp.exp(score), 0.0)
        sums[pl.ds(r, 1), :] = jnp.sum(grown, axis=0, keepdims=True)
        marks = jnp.broadcast_to(lab[pl.ds(r, 1), :], (32, 512))
        picks[pl.ds(r, 1), :] = jnp.sum(jnp.where(kind == marks, score, 0.0), axis=0, keepdims=True)
        for block in range(4):
            tall[block, pl.ds(r * 36, 32), :] = score[:, block * 128 : (block + 1) * 128]
        return carry

    lax.fori_loop(0, 16, finish, 0)
    usable = lab[...] != 255
    terms = jnp.where(usable, jnp.log(sums[...]) - picks[...], 0.0)
    local_total = jnp.sum(terms)
    local_count = jnp.sum(usable.astype(F32))
    sub = lax.broadcasted_iota(jnp.int32, (8, 128), 0)
    loss_rows[pos] = jnp.where(sub == 0, local_total, local_count)

    def loss_copy(ref, slot, index, target):
        return pltpu.make_async_remote_copy(
            src_ref=ref.at[slot], dst_ref=ref.at[slot],
            send_sem=loss_send.at[index], recv_sem=loss_recv.at[index],
            device_id=target, device_id_type=MESH,
        )

    def send_row(k, carry):
        loss_copy(loss_rows, pos, 0, {"rows": lax.rem(pos + k, nr)}).start()
        return carry

    lax.fori_loop(1, nr, send_row, 0)

    for k in range(CLASSES):
        for block in range(4):
            out_ref[0, k, :, block * 128 : (block + 1) * 128] = tall[
                block, pl.ds(k, 16, stride=36), :
            ].astype(BF16)

    tiles_wait(loss_rows.at[pl.ds(0, nr - 1)], loss_recv.at[0])
    loss_batch[bat] = functools.reduce(lambda a, b: a + b, [loss_rows[i] for i in range(nr)])

    def send_batch(k, carry):
        loss_copy(loss_batch, bat, 1, {"batch": lax.rem(bat + k, nb)}).start()
        return carry

    lax.fori_loop(1, nb, send_batch, 0)

    for name in ("t1", "t2", "s", "e", "q"):
        halo_sent(name)
    for layer in range(7):
        tiles_wait(stats.at[layer, pl.ds(0, nr - 1)], stat_send.at[layer])
    tiles_wait(loss_rows.at[pl.ds(0, nr - 1)], loss_send.at[0])
    tiles_wait(loss_batch.at[pl.ds(0, nb - 1)], loss_recv.at[1])
    whole = functools.reduce(lambda a, b: a + b, [loss_batch[i] for i in range(nb)])
    loss_ref[...] = whole[0:1] / jnp.maximum(whole[1:2], 1.0)
    tiles_wait(loss_batch.at[pl.ds(0, nb - 1)], loss_send.at[1])


def solution(mesh):
    nb, nr = mesh.shape["batch"], mesh.shape["rows"]

    def per_device(xq, x8, x16, x32, labels, fw, iw, gain, shift, cw, cb):
        any_spec = pl.BlockSpec(memory_space=pl.ANY)
        vmem = pl.BlockSpec(memory_space=pltpu.VMEM)
        V = pltpu.VMEM
        logits, loss = pl.pallas_call(
            functools.partial(kernel, nb, nr),
            out_shape=(
                jax.ShapeDtypeStruct((1, CLASSES, 16, 512), BF16),
                jax.ShapeDtypeStruct((1, 128), F32),
            ),
            in_specs=[any_spec] * 11,
            out_specs=(vmem, vmem),
            scratch_shapes=[
                V((18, 512, 256), BF16), V((12, 256, 256), BF16), V((10, 128, 256), BF16),
                V((8, 64, 256), BF16), V((16, 512), jnp.int32), V((4, 3, 3, 256, 128), BF16),
                V((3, 3, 3, 128, 128), BF16), V((7, 128), F32), V((7, 128), F32),
                V((128, CLASSES), BF16), V((1, CLASSES), F32),
                V((16, 512, 128), F32), V((10, 256, 128), F32), V((8, 128, 128), F32),
                V((6, 64, 128), F32), V((10, 256, 128), F32), V((8, 128, 128), F32),
                V((10, 256, 128), F32),
                V((8, 128, 128), BF16), V((6, 64, 128), BF16), V((8, 128, 128), BF16),
                V((12, 256, 128), BF16), V((12, 128, 128), BF16), V((12, 256, 128), BF16),
                V((2, 2, 528, 128), F32), V((2, 2, 272, 128), F32), V((2, 4, 144, 128), F32),
                V((2, 6, 80, 128), F32),
                V((128, 128), F32), V((256, 256), BF16), V((256, 512), BF16),
                V((128, 128), F32), V((32, 128), BF16), V((32, 512), F32),
                V((16, 32, 512), F32), V((10, 32, 256), F32), V((10, 32, 512), F32),
                V((16, 512), F32), V((16, 512), F32), V((4, 16 * 36, 128), F32),
                V((7, nr, 8, 128), F32), V((nr, 8, 128), F32), V((nb, 8, 128), F32),
                pltpu.SemaphoreType.DMA((15,)), pltpu.SemaphoreType.DMA((10,)),
                pltpu.SemaphoreType.DMA((10,)), pltpu.SemaphoreType.DMA((7,)),
                pltpu.SemaphoreType.DMA((7,)), pltpu.SemaphoreType.DMA((2,)),
                pltpu.SemaphoreType.DMA((2,)),
            ],
            compiler_params=pltpu.CompilerParams(
                collective_id=0, has_side_effects=True, vmem_limit_bytes=60 * 1024 * 1024
            ),
        )(xq, x8, x16, x32, labels, fw, iw, gain, shift, cw, cb.reshape(1, CLASSES))
        return logits, loss[0, 0]

    batch, rows = "batch", "rows"
    return jax.shard_map(
        per_device, mesh=mesh,
        in_specs=(P(batch, rows, None, None),) * 4 + (P(batch, rows, None),) + (P(),) * 6,
        out_specs=(P(batch, None, rows, None), P()),
        check_vma=False,
    )
```

profile of v0, /device:TPU:1, one launch (start us, length us, event | category | flops | bytes accessed | tf_op | source)
XLA Modules:
  0.0 74.0 jit_solution(10968828027055834479)
XLA Ops:
  0.6 1.4 %copy.13.cw_hbm = bf16[128,19]{1,0:T(8,128)(2,1)} copy(bf16[128,19]{0,1:T(8,128)(2,1)} %param.20) | data formatting | bytes 9728 | tf_op args[9]
  2.0 68.4 %shard_map.122 = (bf16[1,19,16,512]{3,2,1,0:T(8,128)(2,1)}, f32[1,128]{1,0:T(1,128)}) custom-call(bf16[1,16,512,256]{3,2,1,0:T(8,128)(2,1)} %xq_hbm.1, bf16[1,8,256,256]{3,2,1,0:T(8,128)(2,1)} %x8_hbm.1, bf16[1,4,128,256]{3,2,1,0:T(8,128)(2,1)} %x16_hbm.1, bf16[1,2,64,256]{3,2,1,0:T(8,128)(2,1)} %x32_hbm.1, s32[1,16,512]{2,1,0:T(8,128)} %lab_hbm.1, ...), custom_call_target="tpu_custom_call" | custom-call | tf_op jit(solution)/shard_map/pallas_call | solution.py:450
  70.5 1.7 %copy.16 = bf16[1,19,16,512]{3,2,1,0:T(8,128)(2,1)} copy(bf16[1,19,16,512]{3,2,1,0:T(8,128)(2,1)} %get-tuple-element.8) | data formatting | bytes 622592
where the time goes:
time: 74.2 us; the launch traced here: 74 us
  Pallas kernels  68.4 us (92%)
  local copies, waits for them, and re-layouts  3.12 us (4%)
  between operations  2.46 us (3%)
    pallas_call x1, Pallas kernels, per_device(): pl.pallas_call(functools.partial(kernel, nb, nr), out_shape=(jax.ShapeDty...  68.4 us
    unnamed x2, local copies, waits for them, and re-layouts  3.12 us

commit v1 on v0

v1 whole, which is shorter than its diff:
```python
import functools

import jax
import jax.numpy as jnp
from jax import lax
from jax.experimental import pallas as pl
from jax.experimental.pallas import tpu as pltpu
from jax.sharding import PartitionSpec as P

MESH = pl.DeviceIdType.MESH
FLOOR = 0.05
CLASSES = 19
F32 = jnp.float32
BF16 = jnp.bfloat16


def group_total(tile):
    lane = lax.broadcasted_iota(jnp.int32, tile.shape, 1)
    tile = tile + jnp.where(lane % 2 == 0, pltpu.roll(tile, 127, 1), pltpu.roll(tile, 1, 1))
    return tile + jnp.where(lane % 4 < 2, pltpu.roll(tile, 126, 1), pltpu.roll(tile, 2, 1))


def double_matrix(width, out_axis):
    shape = (2 * width, width) if out_axis == 0 else (width, 2 * width)
    out = lax.broadcasted_iota(jnp.int32, shape, out_axis)
    src = lax.broadcasted_iota(jnp.int32, shape, 1 - out_axis)
    half = out // 2
    other = jnp.clip(half + 2 * (out % 2) - 1, 0, width - 1)
    return jnp.where(src == half, 0.75, 0.0) + jnp.where(src == other, 0.25, 0.0)


def kernel(
    nb, nr,
    xq_hbm, x8_hbm, x16_hbm, x32_hbm, lab_hbm, fw_hbm, iw_hbm, gain_hbm, shift_hbm, cw_hbm, cb_hbm,
    out_hbm, loss_ref,
    xq, x8, x16, x32, lab, fw, iw, gain, shift, cw, cb,
    yq, y8, y16, y32, y4, y5, y6,
    a16, a32, a5, in4, in5, in6,
    p512, p256, p128, p64,
    u64, u128, u256, cwf, wct, bias,
    zt, ze, zc, sums, picks, tall, out,
    moms, stats, loss_rows, loss_batch,
    local_sem, halo_send, halo_recv, stat_send, stat_recv, loss_send, loss_recv,
):
    pos = lax.axis_index("rows")
    bat = lax.axis_index("batch")
    last = nr - 1
    scope = jax.named_scope

    def local(src, dst, index):
        return pltpu.make_async_copy(src, dst, local_sem.at[index])

    copies = {
        "fw0": local(fw_hbm.at[0], fw.at[0], 2),
        "xqa": local(xq_hbm.at[0, pl.ds(0, 6)], xq.at[pl.ds(1, 6)], 3),
        "x32": local(x32_hbm.at[0], x32.at[pl.ds(3, 2)], 1),
        "x16": local(x16_hbm.at[0], x16.at[pl.ds(2, 4)], 10),
        "fw3": local(fw_hbm.at[3], fw.at[3], 0),
        "xqb": local(xq_hbm.at[0, pl.ds(6, 10)], xq.at[pl.ds(7, 10)], 4),
        "fw2": local(fw_hbm.at[2], fw.at[2], 9),
        "gain": local(gain_hbm, gain, 5),
        "shift": local(shift_hbm, shift, 6),
        "iw": local(iw_hbm, iw, 11),
        "x8": local(x8_hbm.at[0], x8.at[pl.ds(1, 8)], 13),
        "fw1": local(fw_hbm.at[1], fw.at[1], 12),
        "cw": local(cw_hbm, cw, 7),
        "cb": local(cb_hbm, cb, 8),
        "lab": local(lab_hbm.at[0], lab, 14),
    }

    barrier = pltpu.get_barrier_semaphore()

    def greet_row(k, carry):
        pl.semaphore_signal(
            barrier, inc=1, device_id={"rows": lax.rem(pos + k, nr)}, device_id_type=MESH
        )
        return carry

    def greet_batch(k, carry):
        pl.semaphore_signal(
            barrier, inc=1, device_id={"batch": lax.rem(bat + k, nb)}, device_id_type=MESH
        )
        return carry

    with scope("greet"):
        lax.fori_loop(1, nr, greet_row, 0)
        lax.fori_loop(1, nb, greet_batch, 0)
    with scope("local_start"):
        for copy in copies.values():
            copy.start()

    with scope("constants"):
        m64 = double_matrix(64, 0)
        u64[:, 0:64] = 0.75 * m64
        u64[:, 64:128] = 0.25 * m64
        m128 = double_matrix(128, 0)
        u128[:, 0:128] = (0.75 * m128).astype(BF16)
        u128[:, 128:256] = (0.25 * m128).astype(BF16)
        for scratch, width in ((p512, 512), (p256, 256), (p128, 128), (p64, 64)):
            rows = scratch.shape[2]
            scratch[:, :, :, 0:8, :] = jnp.zeros((2, 2, rows, 8, 128), F32)
            scratch[:, :, :, width + 8 : width + 16, :] = jnp.zeros((2, 2, rows, 8, 128), F32)

        @pl.when(pos == 0)
        def _():
            xq[0] = jnp.zeros_like(xq[0])
            x8[0] = jnp.zeros_like(x8[0])
            x16[0:2] = jnp.zeros_like(x16[0:2])
            x32[0:3] = jnp.zeros_like(x32[0:3])

        @pl.when(pos == 1)
        def _():
            x32[0] = jnp.zeros_like(x32[0])

        @pl.when(pos == last)
        def _():
            xq[17] = jnp.zeros_like(xq[17])
            x8[9] = jnp.zeros_like(x8[9])
            x16[6:8] = jnp.zeros_like(x16[6:8])
            x32[5:8] = jnp.zeros_like(x32[5:8])

        @pl.when(pos == last - 1)
        def _():
            x32[7] = jnp.zeros_like(x32[7])

    with scope("barrier"):
        copies["x32"].wait()
        copies["x16"].wait()
        pl.semaphore_wait(barrier, nr - 1 + nb - 1)

    def remote(src, dst, index, step):
        return pltpu.make_async_remote_copy(
            src_ref=src, dst_ref=dst, send_sem=halo_send.at[index], recv_sem=halo_recv.at[index],
            device_id={"rows": pos + step}, device_id_type=MESH,
        )

    def halos(name, piece=None):
        if name == "t1":
            return (remote(x32.at[pl.ds(3, 2)], x32.at[pl.ds(1, 2)], 0, 1),
                    remote(x32.at[pl.ds(3, 2)], x32.at[pl.ds(5, 2)], 1, -1), 1)
        if name == "t2":
            return (remote(x32.at[pl.ds(4, 1)], x32.at[pl.ds(0, 1)], 2, 2),
                    remote(x32.at[pl.ds(3, 1)], x32.at[pl.ds(7, 1)], 3, -2), 2)
        if name == "s":
            return (remote(x16.at[pl.ds(4, 2)], x16.at[pl.ds(0, 2)], 4, 1),
                    remote(x16.at[pl.ds(2, 2)], x16.at[pl.ds(6, 2)], 5, -1), 1)
        if name == "e":
            return (remote(x8.at[pl.ds(8, 1)], x8.at[pl.ds(0, 1)], 6, 1),
                    remote(x8.at[pl.ds(1, 1)], x8.at[pl.ds(9, 1)], 7, -1), 1)
        if name == "z":
            return (remote(zt.at[7], ze.at[0], 10, 1), remote(zt.at[0], ze.at[1], 11, -1), 1)
        cols = pl.ds(0, 512) if piece is None else pl.ds(piece * 128, 128)
        return (remote(xq.at[16, cols], xq.at[0, cols], 8, 1),
                remote(xq.at[1, cols], xq.at[17, cols], 9, -1), 1)

    def halo_start(name, piece=None):
        down, up, step = halos(name, piece)
        pl.when(pos + step <= last)(down.start)
        pl.when(pos - step >= 0)(up.start)

    def halo_wait(name):
        down, up, step = halos(name)
        pl.when(pos - step >= 0)(down.wait_recv)
        pl.when(pos + step <= last)(up.wait_recv)

    def halo_sent(name):
        down, up, step = halos(name)
        pl.when(pos + step <= last)(down.wait_send)
        pl.when(pos - step >= 0)(up.wait_send)

    with scope("send_ts"):
        halo_start("t1")
        halo_start("t2")
        halo_start("s")

    def column_sum(values):
        pixels = values.shape[0]
        values = values.reshape(pixels // 64, 8, 8, 128)
        return jnp.sum(jnp.sum(values, axis=0), axis=0)

    def conv(layer, x_ref, in_off, w_ref, y_ref, steps, width, pads):
        depth = x_ref.shape[2]

        def multiply(index):
            rows = steps[index][0]
            pad = pads.at[index % 2]
            lhs = jnp.concatenate(
                [jnp.concatenate([x_ref[in_off + row + dr] for row in rows], axis=0)
                 for dr in range(3)], axis=1)
            rhs = jnp.concatenate(
                [jnp.concatenate([w_ref[dr, dc] for dc in range(3)], axis=1) for dr in range(3)],
                axis=0)
            part = jnp.dot(lhs, rhs, preferred_element_type=F32)
            for i, row in enumerate(rows):
                here = slice(i * width, (i + 1) * width)
                pad[0, i, 8 : 8 + width, :] = part[here, 0:128]
                pad[1, i, 8 : 8 + width, :] = part[here, 256:384]
                y_ref[row] = part[here, 128:256]

        def settle(index):
            rows, own, slot = steps[index]
            pad = pads.at[index % 2]
            for i, row in enumerate(rows):
                y_ref[row] = y_ref[row] + pad[0, i, 7 : 7 + width, :] + pad[1, i, 9 : 9 + width, :]
            count = len(own) * width
            total = sum(column_sum(y_ref[row]) for row in own)
            mean = jnp.sum(total, axis=0, keepdims=True) * (1.0 / count)
            square = jnp.zeros((8, 128), F32)
            for row in own:
                off = y_ref[row] - mean
                square = square + column_sum(off * off)
            moms[layer, slot, 0:1, :] = mean
            moms[layer, slot, 1:2, :] = jnp.sum(square, axis=0, keepdims=True)

        multiply(0)
        for index in range(1, len(steps)):
            multiply(index)
            settle(index - 1)
        settle(len(steps) - 1)

    def moments(layer, slots, pixels):
        tiles = [moms[layer, i] for i in range(slots)]
        total = functools.reduce(lambda a, b: a + b, tiles)
        channel = total[0:1] * (1.0 / slots)
        share = pixels // slots
        square = total[1:2]
        for tile in tiles:
            square = square + share * (tile[0:1] - channel) * (tile[0:1] - channel)
        channel = jnp.broadcast_to(channel, (8, 128))
        square = jnp.broadcast_to(square, (8, 128))
        mean = group_total(channel) * 0.25
        square = group_total(square + pixels * (channel - mean) * (channel - mean))
        sub = lax.broadcasted_iota(jnp.int32, (8, 128), 0)
        stats[layer, pos] = jnp.where(sub == 0, mean, square)

        def send(k, carry):
            stat_copy(layer, lax.rem(pos + k, nr)).start()
            return carry

        lax.fori_loop(1, nr, send, 0)

    def stat_copy(layer, peer):
        return pltpu.make_async_remote_copy(
            src_ref=stats.at[layer, pos], dst_ref=stats.at[layer, pos],
            send_sem=stat_send.at[layer], recv_sem=stat_recv.at[layer],
            device_id={"rows": peer}, device_id_type=MESH,
        )

    def tiles_wait(ref, sem):
        pltpu.make_async_copy(ref, ref, sem).wait()

    def scales(layer, pixels):
        local_count = 4 * pixels
        with scope(f"stat_wait{layer}"):
            tiles_wait(stats.at[layer, pl.ds(0, nr - 1)], stat_recv.at[layer])
        every = [stats[layer, i] for i in range(nr)]
        total = functools.reduce(lambda a, b: a + b, every)
        mean = total[0:1] * (1.0 / nr)
        spread = [(tile[0:1] - mean) * (tile[0:1] - mean) for tile in every]
        square = total[1:2] + local_count * functools.reduce(lambda a, b: a + b, spread)
        var = square * (1.0 / (nr * local_count))
        factor = gain[pl.ds(layer, 1), :] * lax.rsqrt(var + FLOOR)
        return mean, factor, shift[pl.ds(layer, 1), :]

    def activate(values, scale):
        mean, factor, offset = scale
        return jnp.maximum((values - mean) * factor + offset, 0.0).astype(BF16)

    def normalize(y_ref, a_ref, scale, rows, top, bottom):
        for r in range(rows):
            a_ref[r] = activate(y_ref[r], scale)

        @pl.when(pos == 0)
        def _():
            a_ref[top] = a_ref[top + 1]

        @pl.when(pos == last)
        def _():
            a_ref[bottom] = a_ref[bottom - 1]

    def double(a_ref, u_ref, in_ref, pairs):
        top_row = a_ref.shape[0] - 1
        end = in_ref.shape[0]
        for k, j in pairs:
            mid = a_ref[k]
            rhs = jnp.concatenate(
                [jnp.concatenate([mid, mid], axis=1),
                 jnp.concatenate([a_ref[max(k - 1, 0)], a_ref[min(k + 1, top_row)]], axis=1)],
                axis=0)
            both = jnp.dot(u_ref[...].astype(BF16), rhs, preferred_element_type=F32).astype(BF16)
            if j >= 0:
                in_ref[j] = both[:, 0:128]
            if j + 1 < end:
                in_ref[j + 1] = both[:, 128:256]

    def clear_outside(in_ref, top_rows, bottom_row):
        @pl.when(pos == 0)
        def _():
            in_ref[0:top_rows] = jnp.zeros_like(in_ref[0:top_rows])

        @pl.when(pos == last)
        def _():
            rest = in_ref.shape[0] - bottom_row
            in_ref[bottom_row:] = jnp.zeros((rest,) + in_ref.shape[1:], BF16)

    nt = (((1,), (1,)), ((), ()))

    def quarter(steps):
        conv(0, xq, 0, fw.at[0], yq, [(rows, rows, slot) for rows, slot in steps], 512, p512)

    with scope("q_wait_a"):
        copies["fw0"].wait()
        copies["xqa"].wait()
    with scope("q_a"):
        quarter([((1, 2), 0), ((3, 4), 1)])
    with scope("q_wait_b"):
        copies["xqb"].wait()
    with scope("q_b"):
        quarter([((5, 6), 2), ((7, 8), 3)])

    with scope("t_wait"):
        copies["fw3"].wait()
        halo_wait("t1")
        halo_wait("t2")
    with scope("l3"):
        conv(3, x32, 0, fw.at[3], y32, [(tuple(range(6)), (2, 3), 0)], 64, p64)
        moments(3, 1, 2 * 64)
    copies["x8"].wait()
    halo_start("e")

    with scope("q_c"):
        quarter([((9, 10), 4), ((11, 12), 5)])

    with scope("s_wait"):
        copies["fw2"].wait()
        halo_wait("s")
    with scope("l2"):
        conv(2, x16, 0, fw.at[2], y16, [(tuple(range(6)), (1, 2, 3, 4), 0)], 128, p128)
        moments(2, 1, 4 * 128)
    halo_start("q", 0)

    copies["gain"].wait()
    copies["shift"].wait()
    copies["iw"].wait()
    scale3 = scales(3, 2 * 64)
    with scope("l5"):
        normalize(y32, a32, scale3, 6, 1, 4)
        double(a32, u64, in5, [(1, 0), (2, 2), (3, 4), (4, 6)])
        clear_outside(in5, 2, 6)
        conv(5, in5, 0, iw.at[1], y5, [(tuple(range(6)), (1, 2, 3, 4), 0)], 128, p128)
        moments(5, 1, 4 * 128)
    halo_start("q", 1)

    with scope("q_d"):
        quarter([((13, 14), 6)])
    halo_start("q", 2)

    eight = [((0, 1, 2, 3),) * 2 + (0,), ((4, 5, 6, 7),) * 2 + (1,)]
    with scope("e_wait"):
        copies["fw1"].wait()
        halo_wait("e")
    with scope("l1"):
        conv(1, x8, 0, fw.at[1], y8, eight, 256, p256)
        moments(1, 2, 8 * 256)
    halo_start("q", 3)

    scale2 = scales(2, 4 * 128)
    five = [(0, -1), (1, 1), (2, 3), (3, 5), (4, 7), (5, 9)]
    with scope("l4"):
        normalize(y16, a16, scale2, 6, 0, 5)
        double(a16, u128, in4, five)
        clear_outside(in4, 1, 9)
        conv(4, in4, 0, iw.at[0], y4, eight, 256, p256)
        moments(4, 2, 8 * 256)

    scale5 = scales(5, 4 * 128)
    with scope("l6"):
        normalize(y5, a5, scale5, 6, 0, 5)
        double(a5, u128, in6, five)
        clear_outside(in6, 1, 9)
        conv(6, in6, 0, iw.at[2], y6, eight, 256, p256)
        moments(6, 2, 8 * 256)

    with scope("q_wait_e"):
        halo_wait("q")
    with scope("q_e"):
        quarter([((0, 15), 7)])
        moments(0, 8, 16 * 512)

    with scope("class_consts"):
        copies["cw"].wait()
        copies["cb"].wait()
        copies["lab"].wait()
        u256[...] = double_matrix(256, 1).astype(BF16)
        cwf[...] = jnp.zeros_like(cwf)
        cwf[0:CLASSES, :] = cw[...].astype(F32)
        wct[:, 0:128] = cwf[0:32, :].astype(BF16)
        wct[:, 128:256] = cwf[0:32, :].astype(BF16)
        cwf[...] = jnp.zeros_like(cwf)
        cwf[0:1, 0:CLASSES] = cb[...]
        bias[...] = jnp.broadcast_to(jnp.transpose(cwf[...])[0:32, 0:1], (32, 128))

    scale1 = scales(1, 8 * 256)
    scale4 = scales(4, 8 * 256)
    with scope("z14"):
        for half in range(2):
            act = jnp.concatenate(
                [jnp.concatenate([activate(y4[r], scale4), activate(y8[r], scale1)], axis=1)
                 for r in range(half * 4, half * 4 + 4)], axis=0)
            part = lax.dot_general(wct[...], act, nt, preferred_element_type=F32)
            for i in range(4):
                zt[half * 4 + i] = part[:, i * 256 : (i + 1) * 256]
    scale6 = scales(6, 8 * 256)
    with scope("z6"):
        for half in range(2):
            act = jnp.concatenate(
                [activate(y6[r], scale6) for r in range(half * 4, half * 4 + 4)], axis=0)
            part = lax.dot_general(wct[:, 0:128], act, nt, preferred_element_type=F32)
            for i in range(4):
                zt[half * 4 + i] = zt[half * 4 + i] + part[:, i * 256 : (i + 1) * 256]

    halo_start("z")

    def widen(flat):
        high = flat.astype(BF16)
        low = (flat - high.astype(F32)).astype(BF16)
        return (jnp.dot(high, u256[...], preferred_element_type=F32)
                + jnp.dot(low, u256[...], preferred_element_type=F32))

    with scope("widen"):
        zc[1:9] = widen(zt[...].reshape(256, 256)).reshape(8, 32, 512)

        @pl.when(pos == 0)
        def _():
            ze[0] = zt[0]

        @pl.when(pos == last)
        def _():
            ze[1] = zt[7]

    scale0 = scales(0, 16 * 512)

    def finish(rows):
        act = jnp.concatenate([activate(yq[r], scale0) for r in rows], axis=0)
        main = lax.dot_general(wct[:, 0:128], act, nt, preferred_element_type=F32)
        kind = lax.broadcasted_iota(jnp.int32, (32, 512), 0)
        offset = jnp.concatenate([bias[...]] * 4, axis=1)
        for i, r in enumerate(rows):
            half = r // 2
            near = half + 2 * (r % 2)
            score = (main[:, i * 512 : (i + 1) * 512] + offset
                     + 0.75 * zc[half + 1] + 0.25 * zc[near])
            grown = jnp.where(kind < CLASSES, jnp.exp(score), 0.0)
            sums[r : r + 1, :] = jnp.sum(grown, axis=0, keepdims=True)
            marks = jnp.broadcast_to(lab[r : r + 1, :], (32, 512))
            picks[r : r + 1, :] = jnp.sum(
                jnp.where(kind == marks, score, 0.0), axis=0, keepdims=True)
            for block in range(4):
                tall[block, r * 36 : r * 36 + 32, :] = score[:, block * 128 : (block + 1) * 128]

    with scope("finish"):
        for r in range(1, 15, 2):
            finish((r, r + 1))
    with scope("z_wait"):
        halo_wait("z")
    with scope("finish_edge"):
        edges = widen(jnp.concatenate([ze[0], ze[1]], axis=0))
        zc[0] = edges[0:32]
        zc[9] = edges[32:64]
        finish((0, 15))

    with scope("loss_terms"):
        usable = lab[...] != 255
        terms = jnp.where(usable, jnp.log(sums[...]) - picks[...], 0.0)
        both = []
        for part in (terms, usable.astype(F32)):
            part = jnp.sum(part, axis=0, keepdims=True)
            both.append(part[:, 0:128] + part[:, 128:256] + part[:, 256:384] + part[:, 384:512])
        sub = lax.broadcasted_iota(jnp.int32, (8, 128), 0)
        loss_rows[pos] = jnp.where(
            sub == 0, jnp.broadcast_to(both[0], (8, 128)), jnp.broadcast_to(both[1], (8, 128)))

    def loss_copy(ref, slot, index, target):
        return pltpu.make_async_remote_copy(
            src_ref=ref.at[slot], dst_ref=ref.at[slot],
            send_sem=loss_send.at[index], recv_sem=loss_recv.at[index],
            device_id=target, device_id_type=MESH,
        )

    def send_row(k, carry):
        loss_copy(loss_rows, pos, 0, {"rows": lax.rem(pos + k, nr)}).start()
        return carry

    lax.fori_loop(1, nr, send_row, 0)

    with scope("scores_out"):
        for k in range(CLASSES):
            for block in range(4):
                out[k, :, block * 128 : (block + 1) * 128] = tall[
                    block, pl.ds(k, 16, stride=36), :
                ].astype(BF16)
        scores_out = local(out, out_hbm.at[0], 15)
        scores_out.start()

    with scope("loss_wait_rows"):
        tiles_wait(loss_rows.at[pl.ds(0, nr - 1)], loss_recv.at[0])
    loss_batch[bat] = functools.reduce(lambda a, b: a + b, [loss_rows[i] for i in range(nr)])

    def send_batch(k, carry):
        loss_copy(loss_batch, bat, 1, {"batch": lax.rem(bat + k, nb)}).start()
        return carry

    lax.fori_loop(1, nb, send_batch, 0)

    with scope("sent_waits"):
        for name in ("t1", "t2", "s", "e", "q", "z"):
            halo_sent(name)
        for layer in range(7):
            tiles_wait(stats.at[layer, pl.ds(0, nr - 1)], stat_send.at[layer])
        tiles_wait(loss_rows.at[pl.ds(0, nr - 1)], loss_send.at[0])
        scores_out.wait()
    with scope("loss_wait_batch"):
        tiles_wait(loss_batch.at[pl.ds(0, nb - 1)], loss_recv.at[1])
    whole = functools.reduce(lambda a, b: a + b, [loss_batch[i] for i in range(nb)])
    whole = jnp.broadcast_to(jnp.sum(whole, axis=1, keepdims=True), (8, 128))
    loss_ref[...] = whole[0:1] / jnp.maximum(whole[1:2], 1.0)
    tiles_wait(loss_batch.at[pl.ds(0, nb - 1)], loss_send.at[1])


def solution(mesh):
    nb, nr = mesh.shape["batch"], mesh.shape["rows"]

    def per_device(xq, x8, x16, x32, labels, fw, iw, gain, shift, cw, cb):
        any_spec = pl.BlockSpec(memory_space=pl.ANY)
        vmem = pl.BlockSpec(memory_space=pltpu.VMEM)
        V = pltpu.VMEM
        dma = pltpu.SemaphoreType.DMA
        logits, loss = pl.pallas_call(
            functools.partial(kernel, nb, nr),
            out_shape=(
                jax.ShapeDtypeStruct((1, CLASSES, 16, 512), BF16),
                jax.ShapeDtypeStruct((1, 128), F32),
            ),
            in_specs=[any_spec] * 11,
            out_specs=(any_spec, vmem),
            scratch_shapes=[
                V((18, 512, 256), BF16), V((10, 256, 256), BF16), V((8, 128, 256), BF16),
                V((8, 64, 256), BF16), V((16, 512), jnp.int32), V((4, 3, 3, 256, 128), BF16),
                V((3, 3, 3, 128, 128), BF16), V((7, 128), F32), V((7, 128), F32),
                V((CLASSES, 128), BF16), V((1, CLASSES), F32),
                V((16, 512, 128), F32), V((8, 256, 128), F32), V((6, 128, 128), F32),
                V((6, 64, 128), F32), V((8, 256, 128), F32), V((6, 128, 128), F32),
                V((8, 256, 128), F32),
                V((6, 128, 128), BF16), V((6, 64, 128), BF16), V((6, 128, 128), BF16),
                V((10, 256, 128), BF16), V((8, 128, 128), BF16), V((10, 256, 128), BF16),
                V((2, 2, 2, 528, 128), F32), V((2, 2, 4, 272, 128), F32),
                V((2, 2, 6, 144, 128), F32), V((2, 2, 6, 80, 128), F32),
                V((128, 128), F32), V((256, 256), BF16), V((256, 512), BF16),
                V((128, 128), F32), V((32, 256), BF16), V((32, 128), F32),
                V((8, 32, 256), F32), V((2, 32, 256), F32), V((10, 32, 512), F32),
                V((16, 512), F32), V((16, 512), F32), V((4, 16 * 36, 128), F32),
                V((CLASSES, 16, 512), BF16),
                V((7, 8, 8, 128), F32), V((7, nr, 8, 128), F32), V((nr, 8, 128), F32),
                V((nb, 8, 128), F32),
                dma((16,)), dma((12,)), dma((12,)), dma((7,)), dma((7,)), dma((2,)), dma((2,)),
            ],
            compiler_params=pltpu.CompilerParams(
                collective_id=0, has_side_effects=True, vmem_limit_bytes=60 * 1024 * 1024
            ),
        )(xq, x8, x16, x32, labels, fw, iw, gain, shift, cw.T, cb.reshape(1, CLASSES))
        return logits, loss[0, 0]

    batch, rows = "batch", "rows"
    return jax.shard_map(
        per_device, mesh=mesh,
        in_specs=(P(batch, rows, None, None),) * 4 + (P(batch, rows, None),) + (P(),) * 6,
        out_specs=(P(batch, None, rows, None), P()),
        check_vma=False,
    )
```

time: 74.2 us -> 52.9 us (0.71)
  Pallas kernels: 68.4 us -> 48.6 us
  local copies, waits for them, and re-layouts: 3.12 us -> 1.71 us
    pallas_call x1, Pallas kernels: 68.4 us -> 48.6 us  [per_device(): pl.pallas_call(functools.partial(kernel, nb, nr), out_shape=(jax.ShapeDty...]
    unnamed x2 -> x1, local copies, waits for them, and re-layouts: 3.12 us -> 1.71 us
where the time goes in v1:
time: 52.9 us; the launch traced here: 52.8 us
  Pallas kernels  48.6 us (92%)
  between operations  2.46 us (5%)
  local copies, waits for them, and re-layouts  1.71 us (3%)
    pallas_call x1, Pallas kernels, per_device(): pl.pallas_call(functools.partial(kernel, nb, nr), out_shape=(jax.ShapeDty...  48.6 us
    unnamed x1, local copies, waits for them, and re-layouts  1.71 us

profile of v1, /device:TPU:1, one launch (start us, length us, event | category | flops | bytes accessed | tf_op | source)
XLA Modules:
  0.0 52.8 jit_solution(6098613165268104394)
XLA Ops:
  0.6 48.6 %shard_map.122 = (bf16[1,19,16,512]{3,2,1,0:T(8,128)(2,1)}, f32[1,128]{1,0:T(1,128)}) custom-call(bf16[1,16,512,256]{3,2,1,0:T(8,128)(2,1)} %xq_hbm.1, bf16[1,8,256,256]{3,2,1,0:T(8,128)(2,1)} %x8_hbm.1, bf16[1,4,128,256]{3,2,1,0:T(8,128)(2,1)} %x16_hbm.1, bf16[1,2,64,256]{3,2,1,0:T(8,128)(2,1)} %x32_hbm.1, s32[1,16,512]{2,1,0:T(8,128)} %lab_hbm.1, ...), custom_call_target="tpu_custom_call" | custom-call | tf_op jit(solution)/shard_map/pallas_call | solution.py:538
  49.2 1.7 %copy.15 = bf16[1,19,16,512]{3,2,1,0:T(8,128)(2,1)} copy(bf16[1,19,16,512]{3,2,1,0:T(8,128)(2,1)} %get-tuple-element.8) | data formatting | bytes 622592

commit v2 on v1

--- a/solution.py
+++ b/solution.py
@@ -32,13 +32,14 @@
 def kernel(
     nb, nr,
     xq_hbm, x8_hbm, x16_hbm, x32_hbm, lab_hbm, fw_hbm, iw_hbm, gain_hbm, shift_hbm, cw_hbm, cb_hbm,
-    out_hbm, loss_ref,
+    out_ref, loss_ref,
     xq, x8, x16, x32, lab, fw, iw, gain, shift, cw, cb,
     yq, y8, y16, y32, y4, y5, y6,
     a16, a32, a5, in4, in5, in6,
     p512, p256, p128, p64,
     u64, u128, u256, cwf, wct, bias,
-    zt, ze, zc, sums, picks, tall, out,
+    zt, ze, z6, zc, sums, picks, tall,
+    wq, w8, w16, w32, wi,
     moms, stats, loss_rows, loss_batch,
     local_sem, halo_send, halo_recv, stat_send, stat_recv, loss_send, loss_recv,
 ):
@@ -70,24 +71,17 @@
 
     barrier = pltpu.get_barrier_semaphore()
 
-    def greet_row(k, carry):
-        pl.semaphore_signal(
-            barrier, inc=1, device_id={"rows": lax.rem(pos + k, nr)}, device_id_type=MESH
-        )
-        return carry
-
-    def greet_batch(k, carry):
-        pl.semaphore_signal(
-            barrier, inc=1, device_id={"batch": lax.rem(bat + k, nb)}, device_id_type=MESH
-        )
-        return carry
-
-    with scope("greet"):
-        lax.fori_loop(1, nr, greet_row, 0)
-        lax.fori_loop(1, nb, greet_batch, 0)
+    def greet(axis, peer):
+        pl.semaphore_signal(barrier, inc=1, device_id={axis: peer}, device_id_type=MESH)
+
     with scope("local_start"):
         for copy in copies.values():
             copy.start()
+    with scope("greet"):
+        for k in sorted(range(1, nr), key=lambda k: -(min(k // 4, 4 - k // 4) + min(k % 4, 4 - k % 4))):
+            greet("rows", lax.rem(pos + k, nr))
+        for k in range(1, nb):
+            greet("batch", lax.rem(bat + k, nb))
 
     with scope("constants"):
         m64 = double_matrix(64, 0)
@@ -123,11 +117,6 @@
         def _():
             x32[7] = jnp.zeros_like(x32[7])
 
-    with scope("barrier"):
-        copies["x32"].wait()
-        copies["x16"].wait()
-        pl.semaphore_wait(barrier, nr - 1 + nb - 1)
-
     def remote(src, dst, index, step):
         return pltpu.make_async_remote_copy(
             src_ref=src, dst_ref=dst, send_sem=halo_send.at[index], recv_sem=halo_recv.at[index],
@@ -135,9 +124,12 @@
         )
 
     def halos(name, piece=None):
+        if name == "t0":
+            return (remote(x32.at[pl.ds(4, 1)], x32.at[pl.ds(2, 1)], 12, 1),
+                    remote(x32.at[pl.ds(3, 1)], x32.at[pl.ds(5, 1)], 13, -1), 1)
         if name == "t1":
-            return (remote(x32.at[pl.ds(3, 2)], x32.at[pl.ds(1, 2)], 0, 1),
-                    remote(x32.at[pl.ds(3, 2)], x32.at[pl.ds(5, 2)], 1, -1), 1)
+            return (remote(x32.at[pl.ds(3, 1)], x32.at[pl.ds(1, 1)], 0, 1),
+                    remote(x32.at[pl.ds(4, 1)], x32.at[pl.ds(6, 1)], 1, -1), 1)
         if name == "t2":
             return (remote(x32.at[pl.ds(4, 1)], x32.at[pl.ds(0, 1)], 2, 2),
                     remote(x32.at[pl.ds(3, 1)], x32.at[pl.ds(7, 1)], 3, -2), 2)
@@ -168,40 +160,54 @@
         pl.when(pos + step <= last)(down.wait_send)
         pl.when(pos - step >= 0)(up.wait_send)
 
-    with scope("send_ts"):
-        halo_start("t1")
-        halo_start("t2")
-        halo_start("s")
-
     def column_sum(values):
         pixels = values.shape[0]
         values = values.reshape(pixels // 64, 8, 8, 128)
         return jnp.sum(jnp.sum(values, axis=0), axis=0)
 
-    def conv(layer, x_ref, in_off, w_ref, y_ref, steps, width, pads):
-        depth = x_ref.shape[2]
-
-        def multiply(index):
-            rows = steps[index][0]
-            pad = pads.at[index % 2]
+    def pair_weights(w_ref, out):
+        depth = w_ref.shape[2]
+        nothing = jnp.zeros((depth, 128), BF16)
+        for t in range(4):
+            out[t * depth : (t + 1) * depth, 0:128] = w_ref[t, 2] if t < 3 else nothing
+            out[t * depth : (t + 1) * depth, 128:256] = w_ref[t - 1, 2] if t > 0 else nothing
+
+    def conv(layer, x_ref, in_off, w_ref, w_pair, y_ref, width, pads):
+        def multiply(step):
+            rows, _, slot = step
+            pad = pads.at[slot % 2]
+            joined = rows[1] == rows[0] + 1
+            taps = 2 if joined else 3
             lhs = jnp.concatenate(
                 [jnp.concatenate([x_ref[in_off + row + dr] for row in rows], axis=0)
                  for dr in range(3)], axis=1)
             rhs = jnp.concatenate(
-                [jnp.concatenate([w_ref[dr, dc] for dc in range(3)], axis=1) for dr in range(3)],
+                [jnp.concatenate([w_ref[dr, dc] for dc in range(taps)], axis=1) for dr in range(3)],
                 axis=0)
             part = jnp.dot(lhs, rhs, preferred_element_type=F32)
             for i, row in enumerate(rows):
                 here = slice(i * width, (i + 1) * width)
                 pad[0, i, 8 : 8 + width, :] = part[here, 0:128]
-                pad[1, i, 8 : 8 + width, :] = part[here, 256:384]
                 y_ref[row] = part[here, 128:256]
-
-        def settle(index):
-            rows, own, slot = steps[index]
-            pad = pads.at[index % 2]
+                if not joined:
+                    pad[1, i, 8 : 8 + width, :] = part[here, 256:384]
+            if joined:
+                lhs = jnp.concatenate(
+                    [jnp.concatenate([x_ref[in_off + row + t] for row in rows[::2]], axis=0)
+                     for t in range(4)], axis=1)
+                part = jnp.dot(lhs, w_pair[...], preferred_element_type=F32)
+                for i in range(len(rows)):
+                    here = slice((i // 2) * width, (i // 2 + 1) * width)
+                    side = slice((i % 2) * 128, (i % 2) * 128 + 128)
+                    pad[1, i, 8 : 8 + width, :] = part[here, side]
+
+        def settle(step):
+            rows, own, slot = step
+            pad = pads.at[slot % 2]
             for i, row in enumerate(rows):
                 y_ref[row] = y_ref[row] + pad[0, i, 7 : 7 + width, :] + pad[1, i, 9 : 9 + width, :]
+            if not own:
+                return
             count = len(own) * width
             total = sum(column_sum(y_ref[row]) for row in own)
             mean = jnp.sum(total, axis=0, keepdims=True) * (1.0 / count)
@@ -212,11 +218,21 @@
             moms[layer, slot, 0:1, :] = mean
             moms[layer, slot, 1:2, :] = jnp.sum(square, axis=0, keepdims=True)
 
-        multiply(0)
-        for index in range(1, len(steps)):
-            multiply(index)
-            settle(index - 1)
-        settle(len(steps) - 1)
+        return multiply, settle
+
+    def run(pieces, steps, before=(), keep=False):
+        multiply, settle = pieces
+        waiting = list(before)
+        for step in steps:
+            multiply(step)
+            for old in waiting:
+                settle(old)
+            waiting = [step]
+        if keep:
+            return waiting
+        for old in waiting:
+            settle(old)
+        return []
 
     def moments(layer, slots, pixels):
         tiles = [moms[layer, i] for i in range(slots)]
@@ -231,7 +247,7 @@
         mean = group_total(channel) * 0.25
         square = group_total(square + pixels * (channel - mean) * (channel - mean))
         sub = lax.broadcasted_iota(jnp.int32, (8, 128), 0)
-        stats[layer, pos] = jnp.where(sub == 0, mean, square)
+        stats[layer, pos] = jnp.where(sub == 0, mean, square)[0:2]
 
         def send(k, carry):
             stat_copy(layer, lax.rem(pos + k, nr)).start()
@@ -305,92 +321,37 @@
 
     nt = (((1,), (1,)), ((), ()))
 
-    def quarter(steps):
-        conv(0, xq, 0, fw.at[0], yq, [(rows, rows, slot) for rows, slot in steps], 512, p512)
+    quarter = conv(0, xq, 0, fw.at[0], wq, yq, 512, p512)
+
+    def band(*firsts):
+        return [((r, r + 1),) * 2 + (r // 2,) for r in firsts]
 
     with scope("q_wait_a"):
         copies["fw0"].wait()
         copies["xqa"].wait()
-    with scope("q_a"):
-        quarter([((1, 2), 0), ((3, 4), 1)])
+    with scope("q_pre"):
+        pair_weights(fw.at[0], wq)
+        late = run(quarter, band(1), keep=True)
+
+    with scope("barrier"):
+        copies["x32"].wait()
+        copies["x16"].wait()
+        pl.semaphore_wait(barrier, nr - 1 + nb - 1)
+    with scope("send_ts"):
+        halo_start("t0")
+        halo_start("s")
+        halo_start("t1")
+
     with scope("q_wait_b"):
         copies["xqb"].wait()
-    with scope("q_b"):
-        quarter([((5, 6), 2), ((7, 8), 3)])
-
-    with scope("t_wait"):
+    with scope("q_a"):
+        late = run(quarter, band(3, 5, 7, 9), late, keep=True)
+
+    with scope("class_consts"):
         copies["fw3"].wait()
-        halo_wait("t1")
-        halo_wait("t2")
-    with scope("l3"):
-        conv(3, x32, 0, fw.at[3], y32, [(tuple(range(6)), (2, 3), 0)], 64, p64)
-        moments(3, 1, 2 * 64)
-    copies["x8"].wait()
-    halo_start("e")
-
-    with scope("q_c"):
-        quarter([((9, 10), 4), ((11, 12), 5)])
-
-    with scope("s_wait"):
-        copies["fw2"].wait()
-        halo_wait("s")
-    with scope("l2"):
-        conv(2, x16, 0, fw.at[2], y16, [(tuple(range(6)), (1, 2, 3, 4), 0)], 128, p128)
-        moments(2, 1, 4 * 128)
-    halo_start("q", 0)
-
-    copies["gain"].wait()
-    copies["shift"].wait()
-    copies["iw"].wait()
-    scale3 = scales(3, 2 * 64)
-    with scope("l5"):
-        normalize(y32, a32, scale3, 6, 1, 4)
-        double(a32, u64, in5, [(1, 0), (2, 2), (3, 4), (4, 6)])
-        clear_outside(in5, 2, 6)
-        conv(5, in5, 0, iw.at[1], y5, [(tuple(range(6)), (1, 2, 3, 4), 0)], 128, p128)
-        moments(5, 1, 4 * 128)
-    halo_start("q", 1)
-
-    with scope("q_d"):
-        quarter([((13, 14), 6)])
-    halo_start("q", 2)
-
-    eight = [((0, 1, 2, 3),) * 2 + (0,), ((4, 5, 6, 7),) * 2 + (1,)]
-    with scope("e_wait"):
-        copies["fw1"].wait()
-        halo_wait("e")
-    with scope("l1"):
-        conv(1, x8, 0, fw.at[1], y8, eight, 256, p256)
-        moments(1, 2, 8 * 256)
-    halo_start("q", 3)
-
-    scale2 = scales(2, 4 * 128)
-    five = [(0, -1), (1, 1), (2, 3), (3, 5), (4, 7), (5, 9)]
-    with scope("l4"):
-        normalize(y16, a16, scale2, 6, 0, 5)
-        double(a16, u128, in4, five)
-        clear_outside(in4, 1, 9)
-        conv(4, in4, 0, iw.at[0], y4, eight, 256, p256)
-        moments(4, 2, 8 * 256)
-
-    scale5 = scales(5, 4 * 128)
-    with scope("l6"):
-        normalize(y5, a5, scale5, 6, 0, 5)
-        double(a5, u128, in6, five)
-        clear_outside(in6, 1, 9)
-        conv(6, in6, 0, iw.at[2], y6, eight, 256, p256)
-        moments(6, 2, 8 * 256)
-
-    with scope("q_wait_e"):
-        halo_wait("q")
-    with scope("q_e"):
-        quarter([((0, 15), 7)])
-        moments(0, 8, 16 * 512)
-
-    with scope("class_consts"):
         copies["cw"].wait()
         copies["cb"].wait()
-        copies["lab"].wait()
+        pair_weights(fw.at[3], w32)
         u256[...] = double_matrix(256, 1).astype(BF16)
         cwf[...] = jnp.zeros_like(cwf)
         cwf[0:CLASSES, :] = cw[...].astype(F32)
@@ -400,6 +361,89 @@
         cwf[0:1, 0:CLASSES] = cb[...]
         bias[...] = jnp.broadcast_to(jnp.transpose(cwf[...])[0:32, 0:1], (32, 128))
 
+    level3 = conv(3, x32, 0, fw.at[3], w32, y32, 64, p64)
+    with scope("t_wait"):
+        halo_wait("t0")
+    with scope("l3"):
+        run(level3, [((2, 3), (2, 3), 0)])
+        moments(3, 1, 2 * 64)
+    copies["x8"].wait()
+    halo_start("t2")
+    halo_start("e")
+
+    with scope("q_b"):
+        late = run(quarter, band(11, 13), late, keep=True)
+        copies["fw2"].wait()
+        copies["fw1"].wait()
+        copies["iw"].wait()
+        pair_weights(fw.at[2], w16)
+        pair_weights(fw.at[1], w8)
+        for i in range(3):
+            pair_weights(iw.at[i], wi.at[i])
+
+    six = tuple(range(6))
+    mid = (1, 2, 3, 4)
+    with scope("s_wait"):
+        halo_wait("s")
+    with scope("l2"):
+        run(conv(2, x16, 0, fw.at[2], w16, y16, 128, p128), [(six, mid, 0)])
+        moments(2, 1, 4 * 128)
+    halo_start("q", 0)
+
+    with scope("t12_wait"):
+        halo_wait("t1")
+        halo_wait("t2")
+        copies["gain"].wait()
+        copies["shift"].wait()
+    with scope("l3_ext"):
+        run(level3, [((0, 1, 4, 5), (), 1)])
+    scale3 = scales(3, 2 * 64)
+    level5 = conv(5, in5, 1, iw.at[1], wi.at[1], y5, 128, p128)
+    with scope("l5"):
+        normalize(y32, a32, scale3, 6, 1, 4)
+        double(a32, u64, in5, [(k, 2 * k) for k in range(6)])
+        clear_outside(in5, 4, 8)
+        run(level5, [((2, 3, 4, 5),) * 2 + (0,)])
+        moments(5, 1, 4 * 128)
+    halo_start("q", 1)
+    halo_start("q", 2)
+    with scope("l5_ext"):
+        run(level5, [((0, 1, 6, 7), (), 1)])
+
+    eight = [((0, 1, 2, 3),) * 2 + (0,), ((4, 5, 6, 7),) * 2 + (1,)]
+    with scope("e_wait"):
+        halo_wait("e")
+    with scope("l1"):
+        run(conv(1, x8, 0, fw.at[1], w8, y8, 256, p256), eight)
+        moments(1, 2, 8 * 256)
+    halo_start("q", 3)
+
+    scale2 = scales(2, 4 * 128)
+    with scope("l4"):
+        normalize(y16, a16, scale2, 6, 0, 5)
+        double(a16, u128, in4, [(k, 2 * k - 1) for k in range(6)])
+        clear_outside(in4, 1, 9)
+        run(conv(4, in4, 0, iw.at[0], wi.at[0], y4, 256, p256), eight)
+        moments(4, 2, 8 * 256)
+
+    scale5 = scales(5, 4 * 128)
+    level6 = conv(6, in6, 0, iw.at[2], wi.at[2], y6, 256, p256)
+    with scope("l6"):
+        normalize(y5, a5, scale5, 8, 1, 6)
+        double(a5, u128, in6, [(k, 2 * k - 2) for k in range(1, 7)])
+        clear_outside(in6, 2, 10)
+        run(level6, [((1, 2, 3, 4),) * 2 + (0,), ((5, 6, 7, 8),) * 2 + (1,)])
+        moments(6, 2, 8 * 256)
+
+    with scope("q_wait_e"):
+        halo_wait("q")
+    with scope("q_e"):
+        run(quarter, [((0, 15), (0, 15), 7)], late)
+        moments(0, 8, 16 * 512)
+        copies["lab"].wait()
+
+    with scope("l6_ext"):
+        run(level6, [((0, 9), (), 2)])
     scale1 = scales(1, 8 * 256)
     scale4 = scales(4, 8 * 256)
     with scope("z14"):
@@ -410,16 +454,15 @@
             part = lax.dot_general(wct[...], act, nt, preferred_element_type=F32)
             for i in range(4):
                 zt[half * 4 + i] = part[:, i * 256 : (i + 1) * 256]
+    halo_start("z")
     scale6 = scales(6, 8 * 256)
     with scope("z6"):
         for half in range(2):
             act = jnp.concatenate(
-                [activate(y6[r], scale6) for r in range(half * 4, half * 4 + 4)], axis=0)
+                [activate(y6[r], scale6) for r in range(half * 5, half * 5 + 5)], axis=0)
             part = lax.dot_general(wct[:, 0:128], act, nt, preferred_element_type=F32)
-            for i in range(4):
-                zt[half * 4 + i] = zt[half * 4 + i] + part[:, i * 256 : (i + 1) * 256]
-
-    halo_start("z")
+            for i in range(5):
+                z6[half * 5 + i] = part[:, i * 256 : (i + 1) * 256]
 
     def widen(flat):
         high = flat.astype(BF16)
@@ -428,15 +471,17 @@
                 + jnp.dot(low, u256[...], preferred_element_type=F32))
 
     with scope("widen"):
-        zc[1:9] = widen(zt[...].reshape(256, 256)).reshape(8, 32, 512)
+        zc[1:9] = widen((zt[...] + z6[1:9]).reshape(256, 256)).reshape(8, 32, 512)
 
         @pl.when(pos == 0)
         def _():
             ze[0] = zt[0]
+            z6[0] = z6[1]
 
         @pl.when(pos == last)
         def _():
             ze[1] = zt[7]
+            z6[9] = z6[8]
 
     scale0 = scales(0, 16 * 512)
 
@@ -464,7 +509,7 @@
     with scope("z_wait"):
         halo_wait("z")
     with scope("finish_edge"):
-        edges = widen(jnp.concatenate([ze[0], ze[1]], axis=0))
+        edges = widen(jnp.concatenate([ze[0] + z6[0], ze[1] + z6[9]], axis=0))
         zc[0] = edges[0:32]
         zc[9] = edges[32:64]
         finish((0, 15))
@@ -478,7 +523,7 @@
             both.append(part[:, 0:128] + part[:, 128:256] + part[:, 256:384] + part[:, 384:512])
         sub = lax.broadcasted_iota(jnp.int32, (8, 128), 0)
         loss_rows[pos] = jnp.where(
-            sub == 0, jnp.broadcast_to(both[0], (8, 128)), jnp.broadcast_to(both[1], (8, 128)))
+            sub == 0, jnp.broadcast_to(both[0], (8, 128)), jnp.broadcast_to(both[1], (8, 128)))[0:2]
 
     def loss_copy(ref, slot, index, target):
         return pltpu.make_async_remote_copy(
@@ -496,11 +541,9 @@
     with scope("scores_out"):
         for k in range(CLASSES):
             for block in range(4):
-                out[k, :, block * 128 : (block + 1) * 128] = tall[
+                out_ref[0, k, :, block * 128 : (block + 1) * 128] = tall[
                     block, pl.ds(k, 16, stride=36), :
                 ].astype(BF16)
-        scores_out = local(out, out_hbm.at[0], 15)
-        scores_out.start()
 
     with scope("loss_wait_rows"):
         tiles_wait(loss_rows.at[pl.ds(0, nr - 1)], loss_recv.at[0])
@@ -513,16 +556,15 @@
     lax.fori_loop(1, nb, send_batch, 0)
 
     with scope("sent_waits"):
-        for name in ("t1", "t2", "s", "e", "q", "z"):
+        for name in ("t0", "t1", "t2", "s", "e", "q", "z"):
             halo_sent(name)
         for layer in range(7):
             tiles_wait(stats.at[layer, pl.ds(0, nr - 1)], stat_send.at[layer])
         tiles_wait(loss_rows.at[pl.ds(0, nr - 1)], loss_send.at[0])
-        scores_out.wait()
     with scope("loss_wait_batch"):
         tiles_wait(loss_batch.at[pl.ds(0, nb - 1)], loss_recv.at[1])
     whole = functools.reduce(lambda a, b: a + b, [loss_batch[i] for i in range(nb)])
-    whole = jnp.broadcast_to(jnp.sum(whole, axis=1, keepdims=True), (8, 128))
+    whole = jnp.broadcast_to(jnp.sum(whole, axis=1, keepdims=True), (2, 128))
     loss_ref[...] = whole[0:1] / jnp.maximum(whole[1:2], 1.0)
     tiles_wait(loss_batch.at[pl.ds(0, nb - 1)], loss_send.at[1])
 
@@ -538,31 +580,33 @@
         logits, loss = pl.pallas_call(
             functools.partial(kernel, nb, nr),
             out_shape=(
-                jax.ShapeDtypeStruct((1, CLASSES, 16, 512), BF16),
-                jax.ShapeDtypeStruct((1, 128), F32),
+                V((1, CLASSES, 16, 512), BF16),
+                V((1, 128), F32),
             ),
             in_specs=[any_spec] * 11,
-            out_specs=(any_spec, vmem),
+            out_specs=(vmem, vmem),
             scratch_shapes=[
                 V((18, 512, 256), BF16), V((10, 256, 256), BF16), V((8, 128, 256), BF16),
                 V((8, 64, 256), BF16), V((16, 512), jnp.int32), V((4, 3, 3, 256, 128), BF16),
                 V((3, 3, 3, 128, 128), BF16), V((7, 128), F32), V((7, 128), F32),
                 V((CLASSES, 128), BF16), V((1, CLASSES), F32),
                 V((16, 512, 128), F32), V((8, 256, 128), F32), V((6, 128, 128), F32),
-                V((6, 64, 128), F32), V((8, 256, 128), F32), V((6, 128, 128), F32),
-                V((8, 256, 128), F32),
-                V((6, 128, 128), BF16), V((6, 64, 128), BF16), V((6, 128, 128), BF16),
-                V((10, 256, 128), BF16), V((8, 128, 128), BF16), V((10, 256, 128), BF16),
+                V((6, 64, 128), F32), V((8, 256, 128), F32), V((8, 128, 128), F32),
+                V((10, 256, 128), F32),
+                V((6, 128, 128), BF16), V((6, 64, 128), BF16), V((8, 128, 128), BF16),
+                V((10, 256, 128), BF16), V((12, 128, 128), BF16), V((12, 256, 128), BF16),
                 V((2, 2, 2, 528, 128), F32), V((2, 2, 4, 272, 128), F32),
                 V((2, 2, 6, 144, 128), F32), V((2, 2, 6, 80, 128), F32),
                 V((128, 128), F32), V((256, 256), BF16), V((256, 512), BF16),
                 V((128, 128), F32), V((32, 256), BF16), V((32, 128), F32),
-                V((8, 32, 256), F32), V((2, 32, 256), F32), V((10, 32, 512), F32),
+                V((8, 32, 256), F32), V((2, 32, 256), F32), V((10, 32, 256), F32),
+                V((10, 32, 512), F32),
                 V((16, 512), F32), V((16, 512), F32), V((4, 16 * 36, 128), F32),
-                V((CLASSES, 16, 512), BF16),
-                V((7, 8, 8, 128), F32), V((7, nr, 8, 128), F32), V((nr, 8, 128), F32),
-                V((nb, 8, 128), F32),
-                dma((16,)), dma((12,)), dma((12,)), dma((7,)), dma((7,)), dma((2,)), dma((2,)),
+                V((1024, 256), BF16), V((1024, 256), BF16), V((1024, 256), BF16),
+                V((1024, 256), BF16), V((3, 512, 256), BF16),
+                V((7, 8, 8, 128), F32), V((7, nr, 2, 128), F32), V((nr, 2, 128), F32),
+                V((nb, 2, 128), F32),
+                dma((15,)), dma((14,)), dma((14,)), dma((7,)), dma((7,)), dma((2,)), dma((2,)),
             ],
             compiler_params=pltpu.CompilerParams(
                 collective_id=0, has_side_effects=True, vmem_limit_bytes=60 * 1024 * 1024

time: 52.9 us -> 46.6 us (0.88)
  Pallas kernels: 48.6 us -> 43.9 us
  local copies, waits for them, and re-layouts: 1.71 us -> 0.72 us
  between operations: 2.46 us -> 1.81 us
    pallas_call x1, Pallas kernels: 48.6 us -> 43.9 us  [per_device(): pl.pallas_call(functools.partial(kernel, nb, nr), out_shape=(V((1, CLASSE...]
    unnamed x1, local copies, waits for them, and re-layouts: 1.71 us -> 0.72 us
where the time goes in v2:
time: 46.6 us; the launch traced here: 46.5 us
  Pallas kernels  43.9 us (94%)
  between operations  1.81 us (4%)
  local copies, waits for them, and re-layouts  0.72 us (2%)
    pallas_call x1, Pallas kernels, per_device(): pl.pallas_call(functools.partial(kernel, nb, nr), out_shape=(V((1, CLASSE...  43.9 us

profile of v2, /device:TPU:1, one launch (start us, length us, event | category | flops | bytes accessed | tf_op | source)
XLA Modules:
  0.0 46.5 jit_solution(13498797480395143926)
XLA Ops:
  0.6 43.9 %shard_map.122 = (bf16[1,19,16,512]{3,2,1,0:T(8,128)(2,1)S(1)}, f32[1,128]{1,0:T(1,128)S(1)}) custom-call(bf16[1,16,512,256]{3,2,1,0:T(8,128)(2,1)} %xq_hbm.1, bf16[1,8,256,256]{3,2,1,0:T(8,128)(2,1)} %x8_hbm.1, bf16[1,4,128,256]{3,2,1,0:T(8,128)(2,1)} %x16_hbm.1, bf16[1,2,64,256]{3,2,1,0:T(8,128)(2,1)} %x32_hbm.1, s32[1,16,512]{2,1,0:T(8,128)} %lab_hbm.1, ...), custom_call_target="tpu_custom_call" | custom-call | tf_op jit(solution)/shard_map/pallas_call | solution.py:580
  44.6 0.7 %copy.15 = bf16[1,19,16,512]{3,2,1,0:T(8,128)(2,1)} copy(bf16[1,19,16,512]{3,2,1,0:T(8,128)(2,1)S(1)} %get-tuple-element.6) | data formatting | bytes 622592

commit v3 on v2

--- a/solution.py
+++ b/solution.py
@@ -14,10 +14,24 @@
 BF16 = jnp.bfloat16
 
 
-def group_total(tile):
-    lane = lax.broadcasted_iota(jnp.int32, tile.shape, 1)
-    tile = tile + jnp.where(lane % 2 == 0, pltpu.roll(tile, 127, 1), pltpu.roll(tile, 1, 1))
-    return tile + jnp.where(lane % 4 < 2, pltpu.roll(tile, 126, 1), pltpu.roll(tile, 2, 1))
+def group_moments(mean, square, count):
+    lane = lax.broadcasted_iota(jnp.int32, mean.shape, 1)
+    for bit in (1, 2):
+        low = lane % (2 * bit) < bit
+
+        def other(tile):
+            return jnp.where(low, pltpu.roll(tile, 128 - bit, 1), pltpu.roll(tile, bit, 1))
+
+        off = mean - other(mean)
+        square = square + other(square) + (count * bit * 0.5) * off * off
+        mean = 0.5 * (mean + other(mean))
+    return mean, square
+
+
+def tree_sum(items):
+    while len(items) > 1:
+        items = [sum(items[i : i + 2][1:], items[i]) for i in range(0, len(items), 2)]
+    return items[0]
 
 
 def double_matrix(width, out_axis):
@@ -37,7 +51,7 @@
     yq, y8, y16, y32, y4, y5, y6,
     a16, a32, a5, in4, in5, in6,
     p512, p256, p128, p64,
-    u64, u128, u256, cwf, wct, bias,
+    u64, u128, u256, cwf, wct, two, bias,
     zt, ze, z6, zc, sums, picks, tall,
     wq, w8, w16, w32, wi,
     moms, stats, loss_rows, loss_batch,
@@ -53,11 +67,11 @@
 
     copies = {
         "fw0": local(fw_hbm.at[0], fw.at[0], 2),
-        "xqa": local(xq_hbm.at[0, pl.ds(0, 6)], xq.at[pl.ds(1, 6)], 3),
+        "xqa": local(xq_hbm.at[0, pl.ds(0, 4)], xq.at[pl.ds(1, 4)], 3),
         "x32": local(x32_hbm.at[0], x32.at[pl.ds(3, 2)], 1),
         "x16": local(x16_hbm.at[0], x16.at[pl.ds(2, 4)], 10),
         "fw3": local(fw_hbm.at[3], fw.at[3], 0),
-        "xqb": local(xq_hbm.at[0, pl.ds(6, 10)], xq.at[pl.ds(7, 10)], 4),
+        "xqb": local(xq_hbm.at[0, pl.ds(4, 12)], xq.at[pl.ds(5, 12)], 4),
         "fw2": local(fw_hbm.at[2], fw.at[2], 9),
         "gain": local(gain_hbm, gain, 5),
         "shift": local(shift_hbm, shift, 6),
@@ -71,6 +85,16 @@
 
     barrier = pltpu.get_barrier_semaphore()
 
+    far = sorted(
+        [(dz, dy) for dz in range(4) for dy in range(4) if dz or dy],
+        key=lambda d: -(min(d[0], 4 - d[0]) + min(d[1], 4 - d[1])))
+
+    def row_peers():
+        return [lax.rem(pos // 4 + dz, 4) * 4 + lax.rem(lax.rem(pos, 4) + dy, 4) for dz, dy in far]
+
+    def batch_peers():
+        return [lax.rem(bat + k, nb) for k in sorted(range(1, nb), key=lambda k: -min(k, nb - k))]
+
     def greet(axis, peer):
         pl.semaphore_signal(barrier, inc=1, device_id={axis: peer}, device_id_type=MESH)
 
@@ -78,10 +102,10 @@
         for copy in copies.values():
             copy.start()
     with scope("greet"):
-        for k in sorted(range(1, nr), key=lambda k: -(min(k // 4, 4 - k // 4) + min(k % 4, 4 - k % 4))):
-            greet("rows", lax.rem(pos + k, nr))
-        for k in range(1, nb):
-            greet("batch", lax.rem(bat + k, nb))
+        for peer in row_peers():
+            greet("rows", peer)
+        for peer in batch_peers():
+            greet("batch", peer)
 
     with scope("constants"):
         m64 = double_matrix(64, 0)
@@ -133,9 +157,12 @@
         if name == "t2":
             return (remote(x32.at[pl.ds(4, 1)], x32.at[pl.ds(0, 1)], 2, 2),
                     remote(x32.at[pl.ds(3, 1)], x32.at[pl.ds(7, 1)], 3, -2), 2)
-        if name == "s":
-            return (remote(x16.at[pl.ds(4, 2)], x16.at[pl.ds(0, 2)], 4, 1),
-                    remote(x16.at[pl.ds(2, 2)], x16.at[pl.ds(6, 2)], 5, -1), 1)
+        if name == "s0":
+            return (remote(x16.at[pl.ds(5, 1)], x16.at[pl.ds(1, 1)], 4, 1),
+                    remote(x16.at[pl.ds(2, 1)], x16.at[pl.ds(6, 1)], 5, -1), 1)
+        if name == "s1":
+            return (remote(x16.at[pl.ds(4, 1)], x16.at[pl.ds(0, 1)], 14, 1),
+                    remote(x16.at[pl.ds(3, 1)], x16.at[pl.ds(7, 1)], 15, -1), 1)
         if name == "e":
             return (remote(x8.at[pl.ds(8, 1)], x8.at[pl.ds(0, 1)], 6, 1),
                     remote(x8.at[pl.ds(1, 1)], x8.at[pl.ds(9, 1)], 7, -1), 1)
@@ -226,34 +253,27 @@
         for step in steps:
             multiply(step)
             for old in waiting:
-                settle(old)
-            waiting = [step]
+                old()
+            waiting = [functools.partial(settle, step)]
         if keep:
             return waiting
         for old in waiting:
-            settle(old)
+            old()
         return []
 
-    def moments(layer, slots, pixels):
-        tiles = [moms[layer, i] for i in range(slots)]
-        total = functools.reduce(lambda a, b: a + b, tiles)
-        channel = total[0:1] * (1.0 / slots)
-        share = pixels // slots
-        square = total[1:2]
-        for tile in tiles:
-            square = square + share * (tile[0:1] - channel) * (tile[0:1] - channel)
-        channel = jnp.broadcast_to(channel, (8, 128))
-        square = jnp.broadcast_to(square, (8, 128))
-        mean = group_total(channel) * 0.25
-        square = group_total(square + pixels * (channel - mean) * (channel - mean))
+    def moments(layer, counts):
+        pixels = sum(counts)
+        tiles = [moms[layer, i] for i in range(len(counts))]
+        channel = tree_sum([tile[0:1] * (n / pixels) for tile, n in zip(tiles, counts)])
+        off = [tile[0:1] - channel for tile in tiles]
+        square = tree_sum([tile[1:2] + n * (one * one) for tile, n, one in zip(tiles, counts, off)])
+        mean, square = group_moments(
+            jnp.broadcast_to(channel, (8, 128)), jnp.broadcast_to(square, (8, 128)), pixels)
         sub = lax.broadcasted_iota(jnp.int32, (8, 128), 0)
         stats[layer, pos] = jnp.where(sub == 0, mean, square)[0:2]
 
-        def send(k, carry):
-            stat_copy(layer, lax.rem(pos + k, nr)).start()
-            return carry
-
-        lax.fori_loop(1, nr, send, 0)
+        for peer in row_peers():
+            stat_copy(layer, peer).start()
 
     def stat_copy(layer, peer):
         return pltpu.make_async_remote_copy(
@@ -270,54 +290,48 @@
         with scope(f"stat_wait{layer}"):
             tiles_wait(stats.at[layer, pl.ds(0, nr - 1)], stat_recv.at[layer])
         every = [stats[layer, i] for i in range(nr)]
-        total = functools.reduce(lambda a, b: a + b, every)
+        total = tree_sum(every)
         mean = total[0:1] * (1.0 / nr)
-        spread = [(tile[0:1] - mean) * (tile[0:1] - mean) for tile in every]
-        square = total[1:2] + local_count * functools.reduce(lambda a, b: a + b, spread)
+        off = [tile[0:1] - mean for tile in every]
+        square = total[1:2] + local_count * tree_sum([one * one for one in off])
         var = square * (1.0 / (nr * local_count))
         factor = gain[pl.ds(layer, 1), :] * lax.rsqrt(var + FLOOR)
-        return mean, factor, shift[pl.ds(layer, 1), :]
+        return factor, shift[pl.ds(layer, 1), :] - mean * factor
+
+    def active(values, scale):
+        return jnp.maximum(values * scale[0] + scale[1], 0.0)
 
     def activate(values, scale):
-        mean, factor, offset = scale
-        return jnp.maximum((values - mean) * factor + offset, 0.0).astype(BF16)
+        return active(values, scale).astype(BF16)
+
+    at_top = jnp.where(pos == 0, 1.0, 0.0).astype(F32)
+    at_end = jnp.where(pos == last, 1.0, 0.0).astype(F32)
 
     def normalize(y_ref, a_ref, scale, rows, top, bottom):
         for r in range(rows):
-            a_ref[r] = activate(y_ref[r], scale)
-
-        @pl.when(pos == 0)
-        def _():
-            a_ref[top] = a_ref[top + 1]
-
-        @pl.when(pos == last)
-        def _():
-            a_ref[bottom] = a_ref[bottom - 1]
-
-    def double(a_ref, u_ref, in_ref, pairs):
+            value = active(y_ref[r], scale)
+            if r == top:
+                value = at_top * active(y_ref[r + 1], scale) + (1.0 - at_top) * value
+            if r == bottom:
+                value = at_end * active(y_ref[r - 1], scale) + (1.0 - at_end) * value
+            a_ref[r] = value.astype(BF16)
+
+    def double(a_ref, u_ref, in_ref, pairs, top_rows, bottom_row):
         top_row = a_ref.shape[0] - 1
-        end = in_ref.shape[0]
         for k, j in pairs:
             mid = a_ref[k]
             rhs = jnp.concatenate(
                 [jnp.concatenate([mid, mid], axis=1),
                  jnp.concatenate([a_ref[max(k - 1, 0)], a_ref[min(k + 1, top_row)]], axis=1)],
                 axis=0)
-            both = jnp.dot(u_ref[...].astype(BF16), rhs, preferred_element_type=F32).astype(BF16)
-            if j >= 0:
-                in_ref[j] = both[:, 0:128]
-            if j + 1 < end:
-                in_ref[j + 1] = both[:, 128:256]
-
-    def clear_outside(in_ref, top_rows, bottom_row):
-        @pl.when(pos == 0)
-        def _():
-            in_ref[0:top_rows] = jnp.zeros_like(in_ref[0:top_rows])
-
-        @pl.when(pos == last)
-        def _():
-            rest = in_ref.shape[0] - bottom_row
-            in_ref[bottom_row:] = jnp.zeros((rest,) + in_ref.shape[1:], BF16)
+            both = jnp.dot(u_ref[...].astype(BF16), rhs, preferred_element_type=F32)
+            for row, value in ((j, both[:, 0:128]), (j + 1, both[:, 128:256])):
+                if 0 <= row < in_ref.shape[0]:
+                    if row < top_rows:
+                        value = (1.0 - at_top) * value
+                    if row >= bottom_row:
+                        value = (1.0 - at_end) * value
+                    in_ref[row] = value.astype(BF16)
 
     nt = (((1,), (1,)), ((), ()))
 
@@ -325,6 +339,18 @@
 
     def band(*firsts):
         return [((r, r + 1),) * 2 + (r // 2,) for r in firsts]
+
+    def edge_rows(taps, fresh):
+        pad = p512.at[1]
+        for i, row in enumerate((0, 15)):
+            lhs = jnp.concatenate([xq[row + dr] for dr in taps[i]], axis=1)
+            rhs = jnp.concatenate(
+                [jnp.concatenate([fw[0, dr, dc] for dc in range(3)], axis=1) for dr in taps[i]],
+                axis=0)
+            part = jnp.dot(lhs, rhs, preferred_element_type=F32)
+            pad[0, i, 8:520, :] = part[:, 0:128]
+            pad[1, i, 8:520, :] = part[:, 256:384]
+            yq[row] = part[:, 128:256] if fresh else yq[row] + part[:, 128:256]
 
     with scope("q_wait_a"):
         copies["fw0"].wait()
@@ -339,8 +365,9 @@
         pl.semaphore_wait(barrier, nr - 1 + nb - 1)
     with scope("send_ts"):
         halo_start("t0")
-        halo_start("s")
+        halo_start("s0")
         halo_start("t1")
+        halo_start("t2")
 
     with scope("q_wait_b"):
         copies["xqb"].wait()
@@ -352,43 +379,55 @@
         copies["cw"].wait()
         copies["cb"].wait()
         pair_weights(fw.at[3], w32)
+        for name in ("fw2", "fw1", "iw"):
+            copies[name].wait()
+        pair_weights(fw.at[2], w16)
+        pair_weights(fw.at[1], w8)
+        for i in range(3):
+            pair_weights(iw.at[i], wi.at[i])
         u256[...] = double_matrix(256, 1).astype(BF16)
         cwf[...] = jnp.zeros_like(cwf)
         cwf[0:CLASSES, :] = cw[...].astype(F32)
         wct[:, 0:128] = cwf[0:32, :].astype(BF16)
         wct[:, 128:256] = cwf[0:32, :].astype(BF16)
+        two[...] = jnp.zeros_like(two)
+        two[0:32, 0:128] = cwf[0:32, :].astype(BF16)
+        two[32:64, 128:256] = cwf[0:32, :].astype(BF16)
         cwf[...] = jnp.zeros_like(cwf)
         cwf[0:1, 0:CLASSES] = cb[...]
-        bias[...] = jnp.broadcast_to(jnp.transpose(cwf[...])[0:32, 0:1], (32, 128))
+        bias[...] = jnp.broadcast_to(jnp.transpose(cwf[...])[0:24, 0:1], (24, 128))
 
     level3 = conv(3, x32, 0, fw.at[3], w32, y32, 64, p64)
     with scope("t_wait"):
         halo_wait("t0")
     with scope("l3"):
         run(level3, [((2, 3), (2, 3), 0)])
-        moments(3, 1, 2 * 64)
+        moments(3, [2 * 64])
     copies["x8"].wait()
-    halo_start("t2")
+    halo_start("s1")
     halo_start("e")
 
     with scope("q_b"):
-        late = run(quarter, band(11, 13), late, keep=True)
-        copies["fw2"].wait()
-        copies["fw1"].wait()
-        copies["iw"].wait()
-        pair_weights(fw.at[2], w16)
-        pair_weights(fw.at[1], w8)
-        for i in range(3):
-            pair_weights(iw.at[i], wi.at[i])
-
-    six = tuple(range(6))
-    mid = (1, 2, 3, 4)
+        late = run(quarter, band(11), late, keep=True)
+
+    level2 = conv(2, x16, 0, fw.at[2], w16, y16, 128, p128)
     with scope("s_wait"):
-        halo_wait("s")
+        halo_wait("s0")
     with scope("l2"):
-        run(conv(2, x16, 0, fw.at[2], w16, y16, 128, p128), [(six, mid, 0)])
-        moments(2, 1, 4 * 128)
-    halo_start("q", 0)
+        level2[0](((1, 2), (1, 2), 0))
+        level2[0](((3, 4), (3, 4), 1))
+
+    with scope("q_c"):
+        quarter[0](band(13)[0])
+        for old in late:
+            old()
+        level2[1](((1, 2), (1, 2), 0))
+        level2[1](((3, 4), (3, 4), 1))
+        moments(2, [256, 256])
+        halo_start("q", 0)
+        edge_rows(((1, 2), (0, 1)), True)
+        quarter[1](band(13)[0])
+        quarter[1](((0, 15), (), 7))
 
     with scope("t12_wait"):
         halo_wait("t1")
@@ -401,49 +440,73 @@
     level5 = conv(5, in5, 1, iw.at[1], wi.at[1], y5, 128, p128)
     with scope("l5"):
         normalize(y32, a32, scale3, 6, 1, 4)
-        double(a32, u64, in5, [(k, 2 * k) for k in range(6)])
-        clear_outside(in5, 4, 8)
-        run(level5, [((2, 3, 4, 5),) * 2 + (0,)])
-        moments(5, 1, 4 * 128)
+        double(a32, u64, in5, [(k, 2 * k) for k in range(1, 5)], 4, 8)
+        run(level5, [((2, 3),) * 2 + (0,), ((4, 5),) * 2 + (1,)])
+        moments(5, [256, 256])
     halo_start("q", 1)
     halo_start("q", 2)
-    with scope("l5_ext"):
-        run(level5, [((0, 1, 6, 7), (), 1)])
-
-    eight = [((0, 1, 2, 3),) * 2 + (0,), ((4, 5, 6, 7),) * 2 + (1,)]
+    level1 = conv(1, x8, 0, fw.at[1], w8, y8, 256, p256)
+    level4 = conv(4, in4, 0, iw.at[0], wi.at[0], y4, 256, p256)
+    inner = [((1, 2, 3, 4),) * 2 + (0,), ((5, 6),) * 2 + (1,), ((0, 7),) * 2 + (2,)]
+    eight = [((0, 1, 2, 3),) * 2 + (0,), ((4, 5),) * 2 + (1,), ((6, 7),) * 2 + (2,)]
+    with scope("l5_ext_l1"):
+        double(a32, u64, in5, [(0, 0), (5, 10)], 4, 8)
+        level5[0](((0, 1, 6, 7), (), 0))
+        level1[0](inner[0])
+        level5[1](((0, 1, 6, 7), (), 0))
+        level1[0](inner[1])
+        level1[1](inner[0])
+
+    with scope("s1_wait"):
+        halo_wait("s1")
+        halo_start("q", 3)
+    with scope("l2_ext"):
+        level2[0](((0, 5), (), 0))
+        level1[1](inner[1])
+        level2[1](((0, 5), (), 0))
     with scope("e_wait"):
         halo_wait("e")
-    with scope("l1"):
-        run(conv(1, x8, 0, fw.at[1], w8, y8, 256, p256), eight)
-        moments(1, 2, 8 * 256)
-    halo_start("q", 3)
-
+    with scope("l1_edge"):
+        run(level1, inner[2:])
+        moments(1, [1024, 512, 512])
     scale2 = scales(2, 4 * 128)
     with scope("l4"):
         normalize(y16, a16, scale2, 6, 0, 5)
-        double(a16, u128, in4, [(k, 2 * k - 1) for k in range(6)])
-        clear_outside(in4, 1, 9)
-        run(conv(4, in4, 0, iw.at[0], wi.at[0], y4, 256, p256), eight)
-        moments(4, 2, 8 * 256)
+        double(a16, u128, in4, [(k, 2 * k - 1) for k in range(4)], 1, 9)
+        level4[0](eight[0])
+        double(a16, u128, in4, [(k, 2 * k - 1) for k in range(4, 6)], 1, 9)
+        level4[0](eight[1])
+        level4[1](eight[0])
+        level4[0](eight[2])
+        level4[1](eight[1])
+        level4[1](eight[2])
+        moments(4, [1024, 512, 512])
 
     scale5 = scales(5, 4 * 128)
     level6 = conv(6, in6, 0, iw.at[2], wi.at[2], y6, 256, p256)
     with scope("l6"):
         normalize(y5, a5, scale5, 8, 1, 6)
-        double(a5, u128, in6, [(k, 2 * k - 2) for k in range(1, 7)])
-        clear_outside(in6, 2, 10)
-        run(level6, [((1, 2, 3, 4),) * 2 + (0,), ((5, 6, 7, 8),) * 2 + (1,)])
-        moments(6, 2, 8 * 256)
+        double(a5, u128, in6, [(k, 2 * k - 2) for k in range(1, 5)], 2, 10)
+        own = [((1, 2, 3, 4),) * 2 + (0,), ((5, 6),) * 2 + (1,), ((7, 8),) * 2 + (2,)]
+        level6[0](own[0])
+        double(a5, u128, in6, [(k, 2 * k - 2) for k in range(5, 7)], 2, 10)
+        level6[0](own[1])
+        level6[1](own[0])
+        level6[0](own[2])
+        level6[1](own[1])
+        level6[1](own[2])
+        moments(6, [1024, 512, 512])
 
     with scope("q_wait_e"):
         halo_wait("q")
     with scope("q_e"):
-        run(quarter, [((0, 15), (0, 15), 7)], late)
-        moments(0, 8, 16 * 512)
+        edge_rows(((0,), (2,)), False)
+        quarter[1](((0, 15), (0, 15), 7))
+        moments(0, [1024] * 8)
         copies["lab"].wait()
 
     with scope("l6_ext"):
-        run(level6, [((0, 9), (), 2)])
+        run(level6, [((0, 9), (), 1)])
     scale1 = scales(1, 8 * 256)
     scale4 = scales(4, 8 * 256)
     with scope("z14"):
@@ -453,16 +516,16 @@
                  for r in range(half * 4, half * 4 + 4)], axis=0)
             part = lax.dot_general(wct[...], act, nt, preferred_element_type=F32)
             for i in range(4):
-                zt[half * 4 + i] = part[:, i * 256 : (i + 1) * 256]
+                zt[half * 4 + i] = part[0:24, i * 256 : (i + 1) * 256]
     halo_start("z")
     scale6 = scales(6, 8 * 256)
     with scope("z6"):
-        for half in range(2):
-            act = jnp.concatenate(
-                [activate(y6[r], scale6) for r in range(half * 5, half * 5 + 5)], axis=0)
-            part = lax.dot_general(wct[:, 0:128], act, nt, preferred_element_type=F32)
-            for i in range(5):
-                z6[half * 5 + i] = part[:, i * 256 : (i + 1) * 256]
+        act = jnp.concatenate(
+            [jnp.concatenate([activate(y6[r], scale6), activate(y6[r + 1], scale6)], axis=1)
+             for r in range(0, 10, 2)], axis=0)
+        part = lax.dot_general(two[...], act, nt, preferred_element_type=F32)
+        for r in range(10):
+            z6[r] = part[r % 2 * 32 : r % 2 * 32 + 24, r // 2 * 256 : r // 2 * 256 + 256]
 
     def widen(flat):
         high = flat.astype(BF16)
@@ -471,7 +534,7 @@
                 + jnp.dot(low, u256[...], preferred_element_type=F32))
 
     with scope("widen"):
-        zc[1:9] = widen((zt[...] + z6[1:9]).reshape(256, 256)).reshape(8, 32, 512)
+        zc[1:9] = widen((zt[...] + z6[1:9]).reshape(192, 256)).reshape(8, 24, 512)
 
         @pl.when(pos == 0)
         def _():
@@ -486,22 +549,22 @@
     scale0 = scales(0, 16 * 512)
 
     def finish(rows):
-        act = jnp.concatenate([activate(yq[r], scale0) for r in rows], axis=0)
-        main = lax.dot_general(wct[:, 0:128], act, nt, preferred_element_type=F32)
-        kind = lax.broadcasted_iota(jnp.int32, (32, 512), 0)
+        act = jnp.concatenate([activate(yq[r], scale0) for r in rows], axis=1)
+        main = lax.dot_general(two[...], act, nt, preferred_element_type=F32)
+        kind = lax.broadcasted_iota(jnp.int32, (24, 512), 0)
         offset = jnp.concatenate([bias[...]] * 4, axis=1)
         for i, r in enumerate(rows):
             half = r // 2
             near = half + 2 * (r % 2)
-            score = (main[:, i * 512 : (i + 1) * 512] + offset
+            score = (main[i * 32 : i * 32 + 24] + offset
                      + 0.75 * zc[half + 1] + 0.25 * zc[near])
             grown = jnp.where(kind < CLASSES, jnp.exp(score), 0.0)
             sums[r : r + 1, :] = jnp.sum(grown, axis=0, keepdims=True)
-            marks = jnp.broadcast_to(lab[r : r + 1, :], (32, 512))
+            marks = jnp.broadcast_to(lab[r : r + 1, :], (24, 512))
             picks[r : r + 1, :] = jnp.sum(
                 jnp.where(kind == marks, score, 0.0), axis=0, keepdims=True)
             for block in range(4):
-                tall[block, r * 36 : r * 36 + 32, :] = score[:, block * 128 : (block + 1) * 128]
+                tall[block, r * 36 : r * 36 + 24, :] = score[:, block * 128 : (block + 1) * 128]
 
     with scope("finish"):
         for r in range(1, 15, 2):
@@ -510,8 +573,8 @@
         halo_wait("z")
     with scope("finish_edge"):
         edges = widen(jnp.concatenate([ze[0] + z6[0], ze[1] + z6[9]], axis=0))
-        zc[0] = edges[0:32]
-        zc[9] = edges[32:64]
+        zc[0] = edges[0:24]
+        zc[9] = edges[24:48]
         finish((0, 15))
 
     with scope("loss_terms"):
@@ -532,11 +595,8 @@
             device_id=target, device_id_type=MESH,
         )
 
-    def send_row(k, carry):
-        loss_copy(loss_rows, pos, 0, {"rows": lax.rem(pos + k, nr)}).start()
-        return carry
-
-    lax.fori_loop(1, nr, send_row, 0)
+    for peer in row_peers():
+        loss_copy(loss_rows, pos, 0, {"rows": peer}).start()
 
     with scope("scores_out"):
         for k in range(CLASSES):
@@ -549,14 +609,11 @@
         tiles_wait(loss_rows.at[pl.ds(0, nr - 1)], loss_recv.at[0])
     loss_batch[bat] = functools.reduce(lambda a, b: a + b, [loss_rows[i] for i in range(nr)])
 
-    def send_batch(k, carry):
-        loss_copy(loss_batch, bat, 1, {"batch": lax.rem(bat + k, nb)}).start()
-        return carry
-
-    lax.fori_loop(1, nb, send_batch, 0)
+    for peer in batch_peers():
+        loss_copy(loss_batch, bat, 1, {"batch": peer}).start()
 
     with scope("sent_waits"):
-        for name in ("t0", "t1", "t2", "s", "e", "q", "z"):
+        for name in ("t0", "t1", "t2", "s0", "s1", "e", "q", "z"):
             halo_sent(name)
         for layer in range(7):
             tiles_wait(stats.at[layer, pl.ds(0, nr - 1)], stat_send.at[layer])
@@ -598,15 +655,15 @@
                 V((2, 2, 2, 528, 128), F32), V((2, 2, 4, 272, 128), F32),
                 V((2, 2, 6, 144, 128), F32), V((2, 2, 6, 80, 128), F32),
                 V((128, 128), F32), V((256, 256), BF16), V((256, 512), BF16),
-                V((128, 128), F32), V((32, 256), BF16), V((32, 128), F32),
-                V((8, 32, 256), F32), V((2, 32, 256), F32), V((10, 32, 256), F32),
-                V((10, 32, 512), F32),
+                V((128, 128), F32), V((32, 256), BF16), V((64, 256), BF16), V((24, 128), F32),
+                V((8, 24, 256), F32), V((2, 24, 256), F32), V((10, 24, 256), F32),
+                V((10, 24, 512), F32),
                 V((16, 512), F32), V((16, 512), F32), V((4, 16 * 36, 128), F32),
                 V((1024, 256), BF16), V((1024, 256), BF16), V((1024, 256), BF16),
                 V((1024, 256), BF16), V((3, 512, 256), BF16),
                 V((7, 8, 8, 128), F32), V((7, nr, 2, 128), F32), V((nr, 2, 128), F32),
                 V((nb, 2, 128), F32),
-                dma((15,)), dma((14,)), dma((14,)), dma((7,)), dma((7,)), dma((2,)), dma((2,)),
+                dma((15,)), dma((16,)), dma((16,)), dma((7,)), dma((7,)), dma((2,)), dma((2,)),
             ],
             compiler_params=pltpu.CompilerParams(
                 collective_id=0, has_side_effects=True, vmem_limit_bytes=60 * 1024 * 1024

time: 46.6 us -> 45 us (0.966)
  Pallas kernels: 43.9 us -> 42.4 us
    pallas_call x1, Pallas kernels: 43.9 us -> 42.4 us  [per_device(): pl.pallas_call(functools.partial(kernel, nb, nr), out_shape=(V((1, CLASSE...]
where the time goes in v3:
time: 45 us; the launch traced here: 44.9 us
  Pallas kernels  42.4 us (94%)
  between operations  1.81 us (4%)
  local copies, waits for them, and re-layouts  0.72 us (2%)
    pallas_call x1, Pallas kernels, per_device(): pl.pallas_call(functools.partial(kernel, nb, nr), out_shape=(V((1, CLASSE...  42.4 us

profile of v3, /device:TPU:1, one launch (start us, length us, event | category | flops | bytes accessed | tf_op | source)
XLA Modules:
  0.0 44.9 jit_solution(13112720902747787454)
XLA Ops:
  0.6 42.4 %shard_map.122 = (bf16[1,19,16,512]{3,2,1,0:T(8,128)(2,1)S(1)}, f32[1,128]{1,0:T(1,128)S(1)}) custom-call(bf16[1,16,512,256]{3,2,1,0:T(8,128)(2,1)} %xq_hbm.1, bf16[1,8,256,256]{3,2,1,0:T(8,128)(2,1)} %x8_hbm.1, bf16[1,4,128,256]{3,2,1,0:T(8,128)(2,1)} %x16_hbm.1, bf16[1,2,64,256]{3,2,1,0:T(8,128)(2,1)} %x32_hbm.1, s32[1,16,512]{2,1,0:T(8,128)} %lab_hbm.1, ...), custom_call_target="tpu_custom_call" | custom-call | tf_op jit(solution)/shard_map/pallas_call | solution.py:637
  43.0 0.7 %copy.15 = bf16[1,19,16,512]{3,2,1,0:T(8,128)(2,1)} copy(bf16[1,19,16,512]{3,2,1,0:T(8,128)(2,1)S(1)} %get-tuple-element.6) | data formatting | bytes 622592
